TPU v7x, 256 devices: a whole 4x4x8 slice. The times are simulated.
256 devices in a mesh: seq: 32 (over y_lo, z, core), batch: 8 (over x, y_hi).
Axes of the slice: x: 4, y: 4 (y_hi: 2, y_lo: 2; y = y_hi * 2 + y_lo), z: 8, core: 2. Of those that a mesh axis runs over, the one named last changes fastest.
Arguments:
- embedded: bfloat16 [32768, 1024], P(('batch', 'seq')), parts along dimension 0, may hold values from -6 to 6
- w_qkv: bfloat16 [2, 1024, 3072], P(None, 'seq'), may hold values from -0.1875 to 0.1875
- w_out: bfloat16 [2, 1024, 1024], P(None, 'seq'), may hold values from -0.1875 to 0.1875
- w_pos: bfloat16 [2, 1024, 1024], P(None, None, 'seq'), may hold values from -0.1875 to 0.1875
- bias_content: float32 [2, 1024], replicated, may hold values from -3 to 3
- bias_position: float32 [2, 1024], replicated, may hold values from -3 to 3
- norm_gain: float32 [2, 1024], replicated, may hold values from 0.5 to 1.5
- norm_offset: float32 [2, 1024], replicated, may hold values from -2 to 2
- table: bfloat16 [12288, 1024], P('seq'), may hold values from -1 to 1
- targets: int32 [32768], P('batch'), parts along dimension 0, may hold values from 0 to 12287
- valid_length: int32 [8], P('batch'), parts along dimension 0, may hold values from 3969 to 4096
Outputs:
- hidden_out: bfloat16 [32768, 1024], P(('batch', 'seq')), parts along dimension 0
- token_loss: float32 [32768], P(('batch', 'seq')), parts along dimension 0
- loss_value: float32 [8], P('batch'), parts along dimension 0
There are 8 independent parts, one for each index of `batch`. A program takes and returns all parts, laid end to end along the dimension named above; an argument that names none is the same for every part. Nothing has to cross between parts.
All inputs are finite; a program needn't handle non-finite values.
Results may differ from a plain program's by a relative error of at most 0.006.
Values may be sent and summed in bfloat16 or wider, within the bound.
A program may use at most 64 MiB of HBM per device.

v0:
```python
import jax
import jax.numpy as jnp
from jax import lax
from jax.sharding import PartitionSpec as P

HEADS = 16
LAYERS = 2


norm_eps = 1e-05


def passed_along(x, axis, by):
    devices = lax.axis_size(axis)
    pairs = [(i, i + by) for i in range(devices) if 0 <= i + by < devices]
    return lax.ppermute(x, axis, pairs)


def copy_for_each(x, axis):
    devices = lax.axis_size(axis)
    return lax.all_to_all(jnp.broadcast_to(x[None], (devices, *x.shape)), axis, 0, 0, tiled=True)


def in_order(tiles, dim):
    tiles = jnp.moveaxis(tiles, 0, dim)
    dims = tiles.shape
    return tiles.reshape(*dims[:dim], dims[dim] * dims[dim + 1], *dims[dim + 2 :])


def gather_directly(x, axis, dim):
    tiles = copy_for_each(x, axis)
    return in_order(tiles, dim)


def of_everyone(x, axis):
    return copy_for_each(x, axis).astype(jnp.float32).sum(axis=0)


def sinusoid(row_count, model_width):
    distance = jnp.arange(row_count - 1, -1, -1).astype(jnp.float32)
    inverse = 1.0 / 10000.0 ** (jnp.arange(0, model_width, 2).astype(jnp.float32) / model_width)
    angles = distance[:, None] * inverse[None, :]
    return jnp.concatenate([jnp.sin(angles), jnp.cos(angles)], axis=1).astype(jnp.bfloat16)


def rel_shift(scores):
    leading = scores.shape[:-2]
    row_count, col_count = (scores.shape[-2], scores.shape[-1])
    padded = jnp.pad(scores, [(0, 0)] * len(leading) + [(0, 0), (1, 0)])
    flattened = padded.reshape(leading + (row_count * (col_count + 1),))[..., row_count:]
    return flattened.reshape(leading + (row_count, col_count))


def layer_norm(values, gain_row, offset_row):
    row_mean = jnp.mean(values, -1, keepdims=True)
    centred = values - row_mean
    spread = jnp.mean(centred * centred, -1, keepdims=True)
    return centred * lax.rsqrt(spread + norm_eps) * gain_row + offset_row


def attention_layer(
    hidden,
    qkv_shard,
    out_shard,
    pos_shard,
    content_bias,
    position_bias,
    gain_row,
    offset_row,
    pos_table,
    allowed,
):
    block_len, model_width = hidden.shape
    head_size = model_width // HEADS
    memory = passed_along(hidden, "seq", 1)
    piece_rows = lax.all_gather(qkv_shard, "seq", axis=0, tiled=True)
    own_cols = hidden
    own_part = jnp.dot(own_cols, piece_rows, preferred_element_type=jnp.float32)
    memory_part = jnp.dot(memory, piece_rows[:, model_width:], preferred_element_type=jnp.float32)
    folded = (own_part, memory_part)
    mixed_rows = folded[0]
    key_rows = mixed_rows[:, model_width : 2 * model_width].astype(jnp.bfloat16)
    value_rows = mixed_rows[:, 2 * model_width :].astype(jnp.bfloat16)
    memory_keys = folded[1][:, :model_width].astype(jnp.bfloat16)
    memory_values = folded[1][:, model_width:].astype(jnp.bfloat16)
    pos_share = jnp.dot(pos_table, pos_shard, preferred_element_type=jnp.float32).astype(
        jnp.bfloat16
    )
    pos_keys = gather_directly(pos_share, "seq", 1)
    query_rows = mixed_rows[:, :model_width]
    q_content = (
        (query_rows + content_bias).astype(jnp.bfloat16).reshape(block_len, HEADS, head_size)
    )
    q_position = (
        (query_rows + position_bias).astype(jnp.bfloat16).reshape(block_len, HEADS, head_size)
    )
    keys_all = jnp.concatenate([memory_keys, key_rows], 0).reshape(2 * block_len, HEADS, head_size)
    values_all = jnp.concatenate([memory_values, value_rows], 0).reshape(
        2 * block_len, HEADS, head_size
    )
    content = jnp.einsum("qhd,khd->hqk", q_content, keys_all, preferred_element_type=jnp.float32)
    position = rel_shift(
        jnp.einsum(
            "qhd,khd->hqk",
            q_position,
            pos_keys.reshape(2 * block_len, HEADS, head_size),
            preferred_element_type=jnp.float32,
        )
    )
    scores = (content + position) * head_size ** (-0.5)
    exp_scores = jnp.where(allowed[None], jnp.exp(scores), 0.0)
    attn_probs = (exp_scores / jnp.sum(exp_scores, -1, keepdims=True)).astype(jnp.bfloat16)
    attended = jnp.einsum(
        "hqk,khd->qhd", attn_probs, values_all, preferred_element_type=jnp.float32
    )
    attended = attended.astype(jnp.bfloat16).reshape(block_len, model_width)
    own_cols = attended
    projected = jnp.dot(
        own_cols, gather_directly(out_shard, "seq", 0), preferred_element_type=jnp.float32
    )
    return layer_norm(hidden.astype(jnp.float32) + projected, gain_row, offset_row).astype(
        jnp.bfloat16
    )


def on_device(
    embedded,
    w_qkv,
    w_out,
    w_pos,
    bias_content,
    bias_position,
    norm_gain,
    norm_offset,
    table,
    targets,
    valid_length,
):
    block_len, model_width = embedded.shape
    device_idx = lax.axis_index("seq")
    pos_table = sinusoid(2 * block_len, model_width)
    query_idx = lax.broadcasted_iota(jnp.int32, (block_len, 2 * block_len), 0)
    key_idx = lax.broadcasted_iota(jnp.int32, (block_len, 2 * block_len), 1)
    allowed = (key_idx <= query_idx + block_len) & ((key_idx >= block_len) | (device_idx > 0))
    hidden = embedded
    for layer_idx in range(LAYERS):
        hidden = attention_layer(
            hidden,
            w_qkv[layer_idx],
            w_out[layer_idx],
            w_pos[layer_idx],
            bias_content[layer_idx],
            bias_position[layer_idx],
            norm_gain[layer_idx],
            norm_offset[layer_idx],
            pos_table,
            allowed,
        )
    vocab_first = device_idx * table.shape[0]
    logits = jnp.einsum(
        "td,vd->tv",
        lax.all_gather(hidden, "seq", axis=0, tiled=True),
        table,
        preferred_element_type=jnp.float32,
    )
    exp_sums = jnp.sum(jnp.exp(logits), 1)
    wanted = targets - vocab_first
    columns = lax.broadcasted_iota(jnp.int32, logits.shape, 1)
    picked = jnp.sum(jnp.where(columns == wanted[:, None], logits, 0.0), 1)
    shard_stats = jnp.stack([exp_sums, picked])
    exp_sums, picked = (
        of_everyone(shard_stats[0].astype(jnp.bfloat16), "seq").astype(jnp.float32),
        of_everyone(shard_stats[1].astype(jnp.bfloat16), "seq").astype(jnp.float32),
    )
    doc_length = valid_length[0]
    token_idx = lax.broadcasted_iota(jnp.int32, exp_sums.shape, 0)
    per_token = jnp.where(token_idx < doc_length, jnp.log(exp_sums) - picked, 0.0)
    loss_value = (jnp.sum(per_token) / doc_length.astype(jnp.float32)).reshape(1)
    token_loss = lax.dynamic_slice_in_dim(per_token, device_idx * block_len, block_len)
    own_idx = device_idx * block_len + lax.broadcasted_iota(jnp.int32, (block_len, 1), 0)
    hidden_out = jnp.where(own_idx < doc_length, hidden, jnp.zeros_like(hidden))
    return (hidden_out, token_loss, loss_value)


def solution(mesh):
    in_specs = (
        P(("batch", "seq"), None),
        P(None, "seq", None),
        P(None, "seq", None),
        P(None, None, "seq"),
        P(),
        P(),
        P(),
        P(),
        P("seq", None),
        P("batch"),
        P("batch"),
    )
    out_specs = (P(("batch", "seq"), None), P(("batch", "seq")), P("batch"))
    return jax.shard_map(
        on_device, mesh=mesh, in_specs=in_specs, out_specs=out_specs, check_vma=False
    )
```

profile of v0, /device:TPU:1, one launch (start us, length us, event | category | flops | bytes accessed | tf_op | source)
XLA Modules:
  0.0 378.9 jit_solution(16822463815121106756)
XLA Ops:
  7.2 1.9 fusion.38
  9.2 0.7 all-gather.10.cloned.1.call-update
  9.9 2.2 fusion.18
  12.1 1.1 convolution_convert_fusion.3
  13.2 0.9 broadcast_in_dim.86
  14.1 11.1 %all-to-all-start = ((bf16[32,256,32]{1,2,0:T(8,128)(2,1)}), bf16[32,256,32]{1,2,0:T(8,128)(2,1)S(1)}, u32[]{:S(2)}, u32[]{:S(2)}) async-start(bf16[32,256,32]{1,2,0:T(8,128)(2,1)} %broadcast_in_dim.86), calls=%async_computation | async-start | bytes 1048576 | tf_op jit(solution)/shard_map/all_to_all | solution.py:21
  25.5 21.1 %all-to-all-done = bf16[32,256,32]{1,2,0:T(8,128)(2,1)S(1)} async-done(((bf16[32,256,32]{1,2,0:T(8,128)(2,1)}), bf16[32,256,32]{1,2,0:T(8,128)(2,1)S(1)}, u32[]{:S(2)}, u32[]{:S(2)}) %all-to-all-start) | async-done | bytes 524320 | tf_op jit(solution)/shard_map/all_to_all | solution.py:21
  46.6 0.9 broadcast_in_dim.90
  47.6 5.7 %all-to-all-start.2 = ((bf16[32,256,32]{1,2,0:T(8,128)(2,1)}), bf16[32,256,32]{1,2,0:T(8,128)(2,1)S(1)}, u32[]{:S(2)}, u32[]{:S(2)}) async-start(bf16[32,256,32]{1,2,0:T(8,128)(2,1)} %broadcast_in_dim.90), calls=%async_computation.2 | async-start | bytes 1048576 | tf_op jit(solution)/shard_map/all_to_all | solution.py:21
  53.3 21.1 %all-to-all-done.2 = bf16[32,256,32]{1,2,0:T(8,128)(2,1)S(1)} async-done(((bf16[32,256,32]{1,2,0:T(8,128)(2,1)}), bf16[32,256,32]{1,2,0:T(8,128)(2,1)S(1)}, u32[]{:S(2)}, u32[]{:S(2)}) %all-to-all-start.2) | async-done | bytes 524320 | tf_op jit(solution)/shard_map/all_to_all | solution.py:21
  74.4 1.6 broadcast_in_dim.89
  76.0 6.1 %all-to-all-start.1 = ((bf16[32,32,1024]{2,1,0:T(8,128)(2,1)}), bf16[32,32,1024]{2,1,0:T(8,128)(2,1)}, u32[]{:S(2)}, u32[]{:S(2)}) async-start(bf16[32,32,1024]{2,1,0:T(8,128)(2,1)} %broadcast_in_dim.89), calls=%async_computation.1 | async-start | bytes 4194304 | tf_op jit(solution)/shard_map/all_to_all | solution.py:21
  82.1 4.6 %collective-permute-start = (bf16[128,1024]{1,0:T(8,128)(2,1)S(1)}, bf16[128,1024]{1,0:T(8,128)(2,1)}, u32[]{:S(2)}, u32[]{:S(2)}) collective-permute-start(bf16[128,1024]{1,0:T(8,128)(2,1)S(1)} %copy-done.4), channel_id=1, source_target_pairs={{0,8},{8,16},{16,24},{24,32},{32,40},{40,48},{48,56},{56,64},{64,7... | collective-permute-start | bytes 786440 | tf_op jit(solution)/shard_map/ppermute | solution.py:16
  87.6 24.3 %all-gather.8.cloned.1.call-done = bf16[1,1024,3072]{2,1,0:T(8,128)(2,1)} async-done(((bf16[1,32,3072]{2,1,0:T(8,128)(2,1)}), bf16[1,1024,3072]{2,1,0:T(8,128)(2,1)}) %all-gather.8.cloned.1.call-update) | async-done | bytes 6291472 | tf_op jit(solution)/shard_map/all_gather | solution.py:76
  111.9 3.9 %fusion.43 = (bf16[128,3072]{1,0:T(8,128)(2,1)S(1)}, f32[128,3072]{1,0:T(8,128)S(1)}) fusion(bf16[128,1024]{1,0:T(8,128)(2,1)S(1)} %copy-done.4, bf16[1,1024,3072]{2,1,0:T(8,128)(2,1)} %all-gather.8.cloned.1.call-done), kind=kOutput, calls=%fused_computation.85 | convolution fusion | flops 805699584 | bytes 8912896 | tf_op jit(solution)/shard_map/dot_general | solution.py:78
  115.9 27.7 %collective-permute-done = bf16[128,1024]{1,0:T(8,128)(2,1)} collective-permute-done((bf16[128,1024]{1,0:T(8,128)(2,1)S(1)}, bf16[128,1024]{1,0:T(8,128)(2,1)}, u32[]{:S(2)}, u32[]{:S(2)}) %collective-permute-start) | collective-permute-done | bytes 262176 | tf_op jit(solution)/shard_map/ppermute | solution.py:16
  143.6 1.7 fusion.4
  145.4 1.0 pad_maximum_fusion
  146.4 1.2 copy.50
  147.7 0.9 add_convert_fusion.5
  148.5 1.1 copy.51
  150.2 2.6 pad.7
  152.7 2.9 reshape.161
  155.8 0.6 copy.58
  156.5 1.8 copy.49
  158.3 2.1 copy.48
  160.4 3.0 fusion.15
  163.4 1.7 broadcast_in_dim.92
  165.1 8.6 %all-to-all-start.3 = ((bf16[32,32,1024]{2,1,0:T(8,128)(2,1)}), bf16[32,32,1024]{2,1,0:T(8,128)(2,1)}, u32[]{:S(2)}, u32[]{:S(2)}) async-start(bf16[32,32,1024]{2,1,0:T(8,128)(2,1)} %broadcast_in_dim.92), calls=%async_computation.3 | async-start | bytes 4194304 | tf_op jit(solution)/shard_map/all_to_all | solution.py:21
  173.7 2.9 convolution_convert_fusion.1
  176.7 2.1 fusion.44
  179.2 3.9 %collective-permute-start.1 = (bf16[128,1024]{1,0:T(8,128)(2,1)S(1)}, bf16[128,1024]{1,0:T(8,128)(2,1)}, u32[]{:S(2)}, u32[]{:S(2)}) collective-permute-start(bf16[128,1024]{1,0:T(8,128)(2,1)S(1)} %add_convert_fusion.3), channel_id=1, source_target_pairs={{0,8},{8,16},{16,24},{24,32},{32,40},{40,48},{48,56},{56,64},{64,7... | collective-permute-start | bytes 786440 | tf_op jit(solution)/shard_map/ppermute | solution.py:16
  183.1 16.1 %all-gather.10.cloned.1.call-done = bf16[1,1024,3072]{2,1,0:T(8,128)(2,1)} async-done(((bf16[1,32,3072]{2,1,0:T(8,128)(2,1)}), bf16[1,1024,3072]{2,1,0:T(8,128)(2,1)}) %all-gather.10.cloned.1.call-update) | async-done | bytes 6291472 | tf_op jit(solution)/shard_map/all_gather | solution.py:76
  199.2 4.7 %fusion.45 = (bf16[128,3072]{1,0:T(8,128)(2,1)}, f32[128,3072]{1,0:T(8,128)S(1)}) fusion(bf16[128,1024]{1,0:T(8,128)(2,1)S(1)} %add_convert_fusion.3, bf16[1,1024,3072]{2,1,0:T(8,128)(2,1)} %all-gather.10.cloned.1.call-done), kind=kOutput, calls=%fused_computation.87 | convolution fusion | flops 805699584 | bytes 8912896 | tf_op jit(solution)/shard_map/dot_general | solution.py:78
  203.9 0.8 add_convert_fusion.2
  205.4 2.6 pad.8
  207.9 2.9 reshape.169
  211.0 0.6 copy.59
  211.6 1.1 copy.53
  212.8 1.8 fusion.34
  214.5 12.2 %collective-permute-done.1 = bf16[128,1024]{1,0:T(8,128)(2,1)} collective-permute-done((bf16[128,1024]{1,0:T(8,128)(2,1)S(1)}, bf16[128,1024]{1,0:T(8,128)(2,1)}, u32[]{:S(2)}, u32[]{:S(2)}) %collective-permute-start.1) | collective-permute-done | bytes 262176 | tf_op jit(solution)/shard_map/ppermute | solution.py:16
  226.8 3.0 fusion.7
  229.8 0.7 fusion.36
  230.5 0.8 pad_maximum_fusion.4
  231.3 2.0 copy.54
  233.4 1.9 pad_maximum_fusion.3
  235.2 2.0 copy.52
  237.3 3.0 fusion.12
  240.3 2.9 convolution_convert_fusion
  243.3 2.1 fusion.46
  245.6 1.1 broadcast_select_fusion
  246.8 73.4 %all-gather.6.cloned.1.call-done = bf16[4096,1024]{1,0:T(8,128)(2,1)} async-done(((bf16[128,1024]{1,0:T(8,128)(2,1)}), bf16[4096,1024]{1,0:T(8,128)(2,1)}) %all-gather.6.cloned.1.call-update) | async-done | bytes 8388624 | tf_op jit(solution)/shard_map/all_gather | solution.py:162
  320.2 9.8 %exponential_reduce_fusion = (bf16[4096]{0:T(1024)(128)(2,1)S(1)}, bf16[4096]{0:T(1024)(128)(2,1)S(1)}) fusion(s32[4096]{0:T(1024)S(1)} %broadcast_subtract_fusion, bf16[4096,1024]{1,0:T(8,128)(2,1)} %all-gather.6.cloned.1.call-done, bf16[384,1024]{1,0:T(8,128)(2,1)S(1)} %copy-done), kind=kOutput, calls=%fused_computation.2 | convolution fusion | flops 3227508736 | bytes 9207808 | tf_op jit(solution)/shard_map/td,vd->tv/dot_general | solution.py:160
  330.5 0.5 broadcast.142
  331.0 2.2 reduce.2
  333.2 0.9 reshape.176
  334.1 5.8 %all-to-all-start.5 = ((bf16[32,2,2048]{2,1,0:T(2,128)(2,1)}), bf16[32,2,2048]{2,1,0:T(2,128)(2,1)S(1)}, u32[]{:S(2)}, u32[]{:S(2)}) async-start(bf16[32,2,2048]{2,1,0:T(2,128)(2,1)} %reshape.176), calls=%async_computation.5 | async-start | bytes 524288 | tf_op jit(solution)/shard_map/all_to_all | solution.py:21
  340.4 2.2 reduce.3
  342.6 0.9 reshape.178
  343.4 8.0 %all-to-all-done.5 = bf16[32,2,2048]{2,1,0:T(2,128)(2,1)S(1)} async-done(((bf16[32,2,2048]{2,1,0:T(2,128)(2,1)}), bf16[32,2,2048]{2,1,0:T(2,128)(2,1)S(1)}, u32[]{:S(2)}, u32[]{:S(2)}) %all-to-all-start.5) | async-done | bytes 262176 | tf_op jit(solution)/shard_map/all_to_all | solution.py:21
  351.5 5.4 %all-to-all-start.4 = ((bf16[32,2,2048]{2,1,0:T(2,128)(2,1)}), bf16[32,2,2048]{2,1,0:T(2,128)(2,1)S(1)}, u32[]{:S(2)}, u32[]{:S(2)}) async-start(bf16[32,2,2048]{2,1,0:T(2,128)(2,1)} %reshape.178), calls=%async_computation.4 | async-start | bytes 524288 | tf_op jit(solution)/shard_map/all_to_all | solution.py:21
  357.4 11.3 %all-to-all-done.4 = bf16[32,2,2048]{2,1,0:T(2,128)(2,1)S(1)} async-done(((bf16[32,2,2048]{2,1,0:T(2,128)(2,1)}), bf16[32,2,2048]{2,1,0:T(2,128)(2,1)S(1)}, u32[]{:S(2)}, u32[]{:S(2)}) %all-to-all-start.4) | async-done | bytes 262176 | tf_op jit(solution)/shard_map/all_to_all | solution.py:21
  369.3 0.7 fusion.33
  370.0 0.6 dynamic_slice.3
  (68 shorter events, 4.9 us)
Async XLA Ops:
  7.2 313.0 %copy-start = (bf16[384,1024]{1,0:T(8,128)(2,1)S(1)}, bf16[384,1024]{1,0:T(8,128)(2,1)}, u32[]{:S(2)}) copy-start(bf16[384,1024]{1,0:T(8,128)(2,1)} %param.19) | copy-start | bytes 2359300
  7.2 18.1 %copy-start.13 = (bf16[2,1024,32]{1,2,0:T(8,128)(2,1)S(1)}, bf16[2,1024,32]{1,2,0:T(8,128)(2,1)}, u32[]{:S(2)}) copy-start(bf16[2,1024,32]{1,2,0:T(8,128)(2,1)} %param.14) | copy-start | bytes 393220
  7.2 104.7 %all-gather.8.cloned.1.call-start = ((), (), s32[]{:S(2)}) async-start(), calls=%async_computation.7 | async-start | bytes 6488064 | tf_op jit(solution)/shard_map/all_gather | solution.py:76
  9.1 190.1 %all-gather.10.cloned.1.call-start = ((), (), s32[]{:S(2)}) async-start(), calls=%async_computation.8 | async-start | bytes 6488064 | tf_op jit(solution)/shard_map/all_gather | solution.py:76
  13.2 40.1 %copy-start.7 = (bf16[2,32,1024]{2,1,0:T(8,128)(2,1)S(1)}, bf16[2,32,1024]{2,1,0:T(8,128)(2,1)}, u32[]{:S(2)}) copy-start(bf16[2,32,1024]{2,1,0:T(8,128)(2,1)} %param.13) | copy-start | bytes 393220
  14.1 32.5 %all-to-all-start = ((bf16[32,256,32]{1,2,0:T(8,128)(2,1)}), bf16[32,256,32]{1,2,0:T(8,128)(2,1)S(1)}, u32[]{:S(2)}, u32[]{:S(2)}) async-start(bf16[32,256,32]{1,2,0:T(8,128)(2,1)} %broadcast_in_dim.86), calls=%async_computation | async-start | bytes 1048576 | tf_op jit(solution)/shard_map/all_to_all | solution.py:21
  47.6 26.8 %all-to-all-start.2 = ((bf16[32,256,32]{1,2,0:T(8,128)(2,1)}), bf16[32,256,32]{1,2,0:T(8,128)(2,1)S(1)}, u32[]{:S(2)}, u32[]{:S(2)}) async-start(bf16[32,256,32]{1,2,0:T(8,128)(2,1)} %broadcast_in_dim.90), calls=%async_computation.2 | async-start | bytes 1048576 | tf_op jit(solution)/shard_map/all_to_all | solution.py:21
  74.4 1.6 copy-start.2
  76.0 6.1 %copy-start.4 = (bf16[128,1024]{1,0:T(8,128)(2,1)S(1)}, bf16[128,1024]{1,0:T(8,128)(2,1)}, u32[]{:S(2)}) copy-start(bf16[128,1024]{1,0:T(8,128)(2,1)} %param.11) | copy-start | bytes 786436
  76.0 11.4 %copy-start.9 = (f32[2,1024]{1,0:T(2,128)S(1)}, f32[2,1024]{1,0:T(2,128)}, u32[]{:S(2)}) copy-start(f32[2,1024]{1,0:T(2,128)} %param.15) | copy-start | bytes 24580
  76.0 11.4 %copy-start.10 = (f32[2,1024]{1,0:T(2,128)S(1)}, f32[2,1024]{1,0:T(2,128)}, u32[]{:S(2)}) copy-start(f32[2,1024]{1,0:T(2,128)} %param.16) | copy-start | bytes 24580
  76.0 11.5 %copy-start.11 = (f32[2,1024]{1,0:T(2,128)S(1)}, f32[2,1024]{1,0:T(2,128)}, u32[]{:S(2)}) copy-start(f32[2,1024]{1,0:T(2,128)} %param.17) | copy-start | bytes 24580
  76.0 11.5 %copy-start.12 = (f32[2,1024]{1,0:T(2,128)S(1)}, f32[2,1024]{1,0:T(2,128)}, u32[]{:S(2)}) copy-start(f32[2,1024]{1,0:T(2,128)} %param.18) | copy-start | bytes 24580
  76.0 87.3 %all-to-all-start.1 = ((bf16[32,32,1024]{2,1,0:T(8,128)(2,1)}), bf16[32,32,1024]{2,1,0:T(8,128)(2,1)}, u32[]{:S(2)}, u32[]{:S(2)}) async-start(bf16[32,32,1024]{2,1,0:T(8,128)(2,1)} %broadcast_in_dim.89), calls=%async_computation.1 | async-start | bytes 4194304 | tf_op jit(solution)/shard_map/all_to_all | solution.py:21
  82.1 61.5 %collective-permute-start = (bf16[128,1024]{1,0:T(8,128)(2,1)S(1)}, bf16[128,1024]{1,0:T(8,128)(2,1)}, u32[]{:S(2)}, u32[]{:S(2)}) collective-permute-start(bf16[128,1024]{1,0:T(8,128)(2,1)S(1)} %copy-done.4), channel_id=1, source_target_pairs={{0,8},{8,16},{16,24},{24,32},{32,40},{40,48},{48,56},{56,64},{64,7... | collective-permute-start | bytes 786440 | tf_op jit(solution)/shard_map/ppermute | solution.py:16
  111.9 31.7 %copy-start.1 = (bf16[1,1024,3072]{2,1,0:T(8,128)(2,1)S(1)}, bf16[1,1024,3072]{2,1,0:T(8,128)(2,1)}, u32[]{:S(2)}) copy-start(bf16[1,1024,3072]{2,1,0:T(8,128)(2,1)} %all-gather.8.cloned.1.call-done) | copy-start | bytes 18874372
  165.1 8.7 %copy-start.6 = (bf16[256,1024]{0,1:T(8,128)(2,1)S(1)}, bf16[256,1024]{0,1:T(8,128)(2,1)}, u32[]{:S(2)}) copy-start(bf16[256,1024]{0,1:T(8,128)(2,1)} %copy.48) | copy-start | bytes 1572868
  165.1 78.2 %all-to-all-start.3 = ((bf16[32,32,1024]{2,1,0:T(8,128)(2,1)}), bf16[32,32,1024]{2,1,0:T(8,128)(2,1)}, u32[]{:S(2)}, u32[]{:S(2)}) async-start(bf16[32,32,1024]{2,1,0:T(8,128)(2,1)} %broadcast_in_dim.92), calls=%async_computation.3 | async-start | bytes 4194304 | tf_op jit(solution)/shard_map/all_to_all | solution.py:21
  173.7 146.5 %all-gather.6.cloned.1.call-start = ((), (), s32[]{:S(2)}) async-start(), calls=%async_computation.6 | async-start | bytes 8650752 | tf_op jit(solution)/shard_map/all_gather | solution.py:162
  173.7 2.9 copy-start.5
  179.2 25.6 %copy-start.3 = (bf16[32,256,32]{1,2,0:T(8,128)(2,1)S(1)}, bf16[32,256,32]{1,2,0:T(8,128)(2,1)}, u32[]{:S(2)}) copy-start(bf16[32,256,32]{1,2,0:T(8,128)(2,1)} %copy-done.2) | copy-start | bytes 1572868
  179.2 47.5 %collective-permute-start.1 = (bf16[128,1024]{1,0:T(8,128)(2,1)S(1)}, bf16[128,1024]{1,0:T(8,128)(2,1)}, u32[]{:S(2)}, u32[]{:S(2)}) collective-permute-start(bf16[128,1024]{1,0:T(8,128)(2,1)S(1)} %add_convert_fusion.3), channel_id=1, source_target_pairs={{0,8},{8,16},{16,24},{24,32},{32,40},{40,48},{48,56},{56,64},{64,7... | collective-permute-start | bytes 786440 | tf_op jit(solution)/shard_map/ppermute | solution.py:16
  243.3 3.5 copy-start.8
  334.1 17.4 %all-to-all-start.5 = ((bf16[32,2,2048]{2,1,0:T(2,128)(2,1)}), bf16[32,2,2048]{2,1,0:T(2,128)(2,1)S(1)}, u32[]{:S(2)}, u32[]{:S(2)}) async-start(bf16[32,2,2048]{2,1,0:T(2,128)(2,1)} %reshape.176), calls=%async_computation.5 | async-start | bytes 524288 | tf_op jit(solution)/shard_map/all_to_all | solution.py:21
  351.5 17.3 %all-to-all-start.4 = ((bf16[32,2,2048]{2,1,0:T(2,128)(2,1)}), bf16[32,2,2048]{2,1,0:T(2,128)(2,1)S(1)}, u32[]{:S(2)}, u32[]{:S(2)}) async-start(bf16[32,2,2048]{2,1,0:T(2,128)(2,1)} %reshape.178), calls=%async_computation.4 | async-start | bytes 524288 | tf_op jit(solution)/shard_map/all_to_all | solution.py:21
Sparse Core Ops, SparseCore 0:
  10.4 101.4 all-gather.7
  113.8 85.4 all-gather.9
  246.9 73.2 all-gather.5
where the time goes:
time: 380 us; the launch traced here: 379 us
  waiting for transfers between devices  216 us (57%)
  starting transfers between devices  51.3 us (14%)
  matrix products  41.5 us (11%)
  local copies, waits for them, and re-layouts  38.2 us (10%)
  between operations  16.8 us (4%)
  other arithmetic  15.1 us (4%)
    all_gather x1, waiting for transfers between devices, on_device(): lax.all_gather(hidden, 'seq', axis=0, tiled=True)  73.4 us
    all_to_all x6, waiting for transfers between devices, copy_for_each(): lax.all_to_all(jnp.broadcast_to(x[None], (devices, *x.shape)), axis, 0, 0...  61.5 us
    all_to_all x6, starting transfers between devices, copy_for_each(): lax.all_to_all(jnp.broadcast_to(x[None], (devices, *x.shape)), axis, 0, 0...  42.7 us
    all_gather x2, waiting for transfers between devices, attention_layer(): piece_rows = lax.all_gather(qkv_shard, 'seq', axis=0, tiled=True)  40.4 us
    ppermute x2, waiting for transfers between devices, passed_along(): return lax.ppermute(x, axis, pairs)  40 us
    dot_general x1, matrix products, on_device(): jnp.einsum('td,vd->tv', lax.all_gather(hidden, 'seq', axis=0, tiled=True)...  9.82 us
    dot_general x2, matrix products, attention_layer(): own_part = jnp.dot(own_cols, piece_rows, preferred_element_type=jnp.float32)  8.62 us
    ppermute x2, starting transfers between devices, passed_along(): return lax.ppermute(x, axis, pairs)  8.45 us
  transfers between devices with their start and end apart: 11, of which 9 were waited for; matrix products, arithmetic and copies ran while one was open for 19% of the time, Pallas kernels for 0%

commit v1 on v0

v1 whole, which is shorter than its diff:
```python
import functools

import jax
import jax.numpy as jnp
import numpy as np
from jax import lax
from jax.experimental import pallas as pl
from jax.experimental.pallas import tpu as pltpu
from jax.sharding import PartitionSpec as P

HEADS = 16
LAYERS = 2
D = 1024
BLK = 128
NZ = 8
SHARD = 32
WORDS = 384
PO = 256 + D
EPS = 1e-05
MESH = pl.DeviceIdType.MESH
BF = jnp.bfloat16
F32 = jnp.float32


def pos_table_t(row_count, model_width):
    distance = np.arange(row_count - 1, -1, -1).astype(np.float32)
    inverse = np.float32(1.0) / np.float32(10000.0) ** (
        np.arange(0, model_width, 2).astype(np.float32) / np.float32(model_width)
    )
    angles = distance[:, None] * inverse[None, :].astype(np.float32)
    table = np.concatenate([np.sin(angles), np.cos(angles)], axis=1)
    return jnp.asarray(table.T, F32).astype(BF)


def kernel(
    emb, wqkv, po_in, bias_c, bias_p, gain, offset, table, targets, vlen,
    hid_out, tl_out, loss_out,
    W, POW, T, X0, X1, QC, QP, K, V, ATT, Y, HALL, STL, ST, PART,
    lsem, ring_r, y_r, d_r, w_s, halo_s, halo_r, t_s, t_r, h_s, h_r, st_s, st_r, p_s, p_r,
):
    i = lax.axis_index("seq")
    b = lax.axis_index("batch")
    c = i % 2
    z = (i // 2) % NZ
    y = i // (2 * NZ)
    sgn = 1 - 2 * c

    def dev(yy, zz, cc):
        return (yy * NZ + zz) * 2 + cc

    def zoff(k):
        return (z + 2 * NZ + k) % NZ

    fwd = {"seq": dev(y, zoff(sgn), c)}
    bwd = {"seq": dev(y, zoff(-sgn), c)}
    partner = {"seq": dev(y, z, 1 - c)}
    diag = {"seq": dev(1 - y, z, 1 - c)}
    near = {"seq": dev(1 - y, z, c)}
    far = {"seq": dev(1 - y, z, c), "batch": (b // 2) * 2 + 1 - b % 2}
    nxt = {"seq": (i + 1) % 32}
    prv = {"seq": (i + 31) % 32}

    def rcopy(src, dst, ss, rs, to):
        return pltpu.make_async_remote_copy(
            src_ref=src, dst_ref=dst, send_sem=ss, recv_sem=rs, device_id=to, device_id_type=MESH
        )

    loc = [
        pltpu.make_async_copy(wqkv.at[0], W.at[0, y, z, c], lsem.at[0]),
        pltpu.make_async_copy(emb, X0.at[1], lsem.at[1]),
        pltpu.make_async_copy(po_in, POW.at[:, y, z, c], lsem.at[2]),
        pltpu.make_async_copy(wqkv.at[1], W.at[1, y, z, c], lsem.at[3]),
        pltpu.make_async_copy(table, T.at[y, c], lsem.at[4]),
    ]
    for cp in loc:
        cp.start()

    barrier = pltpu.get_barrier_semaphore()
    for k in range(1, NZ):
        pl.semaphore_signal(barrier, inc=1, device_id={"seq": dev(y, zoff(k), c)}, device_id_type=MESH)
    for peer in (partner, diag, near, far, nxt, prv):
        pl.semaphore_signal(barrier, inc=1, device_id=peer, device_id_type=MESH)
    pl.semaphore_wait(barrier, NZ - 1 + 6)

    def stream(si, yy, zz):
        if si in (3, 7):
            return POW.at[si // 4, yy, zz, c]
        layer, col = (0, si) if si < 3 else (1, si - 4)
        return W.at[layer, yy, zz, c, :, pl.ds(col * D, D)]

    def own(group):
        for si in group:
            s = stream(si, y, z)
            rcopy(s, s, w_s.at[si, 0], ring_r.at[si, 0], fwd).start()
            rcopy(s, s, w_s.at[si, 1], ring_r.at[si, 4], bwd).start()
            rcopy(s, s, w_s.at[si, 2], y_r.at[si, 0], near).start()

    def step(group, d):
        for si in group:
            s = stream(si, y, zoff(-sgn * d))
            rcopy(s, s, w_s.at[si, 0], ring_r.at[si, d - 1], fwd).wait_recv()
            if d < 4:
                rcopy(s, s, w_s.at[si, 0], ring_r.at[si, d], fwd).start()
            rcopy(s, s, w_s.at[si, 3], y_r.at[si, 1], far).start()
            if d < 4:
                s = stream(si, y, zoff(sgn * d))
                rcopy(s, s, w_s.at[si, 1], ring_r.at[si, 3 + d], bwd).wait_recv()
                if d < 3:
                    rcopy(s, s, w_s.at[si, 1], ring_r.at[si, 4 + d], bwd).start()
                rcopy(s, s, w_s.at[si, 2], y_r.at[si, 0], near).start()

    def d2d_own(group):
        for si in group:
            s = stream(si, y, pl.ds(0, NZ))
            rcopy(s, s, w_s.at[si, 4], d_r.at[si, 0], partner).start()

    def d2d_other(group):
        for si in group:
            s4 = stream(si, 1 - y, pl.ds(0, 4))
            rcopy(s4, s4, w_s.at[si, 2], y_r.at[si, 0], near).wait_recv()
            rcopy(s4, s4, w_s.at[si, 3], y_r.at[si, 1], far).wait_recv()
            s = stream(si, 1 - y, pl.ds(0, NZ))
            rcopy(s, s, w_s.at[si, 5], d_r.at[si, 1], partner).start()

    def finish(group):
        for si in group:
            s = stream(si, y, pl.ds(0, NZ))
            rcopy(s, s, w_s.at[si, 4], d_r.at[si, 0], partner).wait_recv()
            rcopy(s, s, w_s.at[si, 5], d_r.at[si, 1], partner).wait_recv()

    def drain(group):
        for si in group:
            for k, n in ((0, 4), (1, 3), (2, 4), (3, 4), (4, 8), (5, 8)):
                s = stream(si, y, pl.ds(0, n))
                rcopy(s, s, w_s.at[si, k], ring_r.at[si, 0], fwd).wait_send()

    low = lax.broadcasted_iota(jnp.int32, (BLK, BLK), 1) < 64
    rows = lax.broadcasted_iota(jnp.int32, (BLK, 2 * BLK), 0)
    cols = lax.broadcasted_iota(jnp.int32, (BLK, 2 * BLK), 1)
    first_key = BLK * (1 - jnp.minimum(i, 1))
    allowed = (cols <= rows + BLK) & (cols >= first_key)

    def lanes(t, size):
        return pl.ds(pl.multiple_of(t * size, size), size)

    def weights(layer, col):
        return W[layer, :, :, :, :, pl.ds(pl.multiple_of(col, 256), 256)].reshape(D, 256)

    def queries(layer, X):
        def body(t, carry):
            sl = lanes(t, 256)
            q = jnp.dot(X[1], weights(layer, t * 256), preferred_element_type=F32)
            QC[:, sl] = (q + bias_c[layer : layer + 1, sl]).astype(BF)
            QP[:, sl] = (q + bias_p[layer : layer + 1, sl]).astype(BF)
            return carry

        lax.fori_loop(0, 4, body, 0)

    def keys_values(layer, X, part):
        row0, count = {"all": (0, 2), "own": (1, 1), "memory": (0, 1)}[part]

        def body(t, carry):
            x = X[row0 : row0 + count].reshape(count * BLK, D)
            r = pl.ds(row0 * BLK, count * BLK)
            sl = lanes(t, 256)
            K[r, sl] = jnp.dot(x, weights(layer, D + t * 256), preferred_element_type=F32).astype(BF)
            V[r, sl] = jnp.dot(x, weights(layer, 2 * D + t * 256), preferred_element_type=F32).astype(BF)
            return carry

        lax.fori_loop(0, 4, body, 0)

    def both(x):
        zero = jnp.zeros_like(x)
        return jnp.concatenate([jnp.where(low, x, zero), jnp.where(low, zero, x)], 0)

    def attend(layer, start, stop):
        def body(p, carry):
            sl = lanes(p, BLK)
            q2 = both(QC[:, sl].astype(F32)).astype(BF)
            r2 = both(QP[:, sl].astype(F32)).astype(BF)
            content = lax.dot_general(
                q2, K[:, sl], (((1,), (1,)), ((), ())), preferred_element_type=F32
            )
            pos = POW[layer, p // 4, pl.ds((p % 4) * 2, 2), :, :, 0:256].reshape(BLK, 2 * BLK)
            position = jnp.dot(r2, pos, preferred_element_type=F32)
            outs = []
            for k in range(2):
                half = slice(k * BLK, (k + 1) * BLK)
                shifted = pltpu.roll(position[half], BLK + 1, 1, stride=1, stride_axis=0)
                scores = (content[half] + shifted) * 0.125
                e = jnp.where(allowed, jnp.exp(scores), 0.0)
                outs.append((e / jnp.sum(e, -1, keepdims=True)).astype(BF))
            o = jnp.dot(jnp.concatenate(outs, 0), V[:, sl], preferred_element_type=F32)
            ATT[:, sl] = jnp.where(low, o[:BLK], o[BLK:]).astype(BF)
            return carry

        lax.fori_loop(start, stop, body, 0)

    def project(layer, X):
        def body(t, carry):
            sl = lanes(t, 256)
            w = POW[layer, :, :, :, :, pl.ds(pl.multiple_of(256 + t * 256, 256), 256)].reshape(D, 256)
            Y[:, sl] = jnp.dot(ATT[...], w, preferred_element_type=F32) + X[1, :, sl].astype(F32)
            return carry

        lax.fori_loop(0, 4, body, 0)

    def norm(layer, dst, last):
        def body(t, carry):
            r = pl.ds(pl.multiple_of(t * 32, 32), 32)
            v = Y[r, :]
            v = v - jnp.mean(v, -1, keepdims=True)
            spread = jnp.mean(v * v, -1, keepdims=True)
            h = v * lax.rsqrt(spread + EPS) * gain[layer : layer + 1, :] + offset[layer : layer + 1, :]
            dst[r, :] = h.astype(BF)
            if last:
                pos = lax.broadcasted_iota(jnp.int32, (32, D), 0) + (i * BLK + t * 32)
                hid_out[r, :] = jnp.where(pos < vlen[0], h, 0.0).astype(BF)
            return carry

        lax.fori_loop(0, 4, body, 0)

    G0, G1, G2 = (0, 1, 2), (3, 4), (5, 6, 7)

    loc[0].wait()
    own(G0)
    loc[1].wait()
    halo0 = rcopy(X0.at[1], X0.at[0], halo_s.at[0], halo_r.at[0], nxt)
    halo0.start()
    for cp in loc[2:]:
        cp.wait()
    for d in (1, 2, 3):
        step(G0, d)
    own(G1)
    step(G0, 4)
    d2d_own(G0)
    step(G1, 1)
    d2d_other(G0)
    halves = (pl.ds(0, WORDS // 2), pl.ds(WORDS // 2, WORDS // 2))
    tcopies = [
        rcopy(T.at[y, c, h], T.at[y, c, h], t_s.at[k], t_r.at[k], to)
        for k, (h, to) in enumerate(zip(halves, (near, far)))
    ] + [rcopy(T.at[y, c], T.at[y, c], t_s.at[2], t_r.at[2], partner)]
    tcopies[2].start()
    finish(G0)
    halo0.wait_recv()
    queries(0, X0)
    step(G1, 2)
    keys_values(0, X0, "all")
    step(G1, 3)
    own(G2)
    step(G1, 4)
    d2d_own(G1)
    d2d_other(G1[:1])
    finish(G1[:1])
    attend(0, 0, 3)
    step(G2, 1)
    attend(0, 3, 6)
    d2d_other(G1[1:])
    attend(0, 6, 8)
    step(G2, 2)
    project(0, X0)
    norm(0, X1.at[1], False)
    halo1 = rcopy(X1.at[1], X1.at[0], halo_s.at[1], halo_r.at[1], nxt)
    halo1.start()
    finish(G1[1:])
    queries(1, X1)
    step(G2, 3)
    step(G2, 4)
    d2d_own(G2)
    tcopies[0].start()
    tcopies[1].start()
    d2d_other(G2)
    finish(G2[:2])
    keys_values(1, X1, "own")
    halo1.wait_recv()
    keys_values(1, X1, "memory")
    finish(G2[2:])
    attend(1, 0, 8)
    tcopies[0].wait_recv()
    tcopies[1].wait_recv()
    t_other = rcopy(T.at[1 - y, c], T.at[1 - y, c], t_s.at[3], t_r.at[3], partner)
    t_other.start()
    project(1, X1)
    norm(1, HALL.at[0], True)

    hv = (pl.ds(0, BLK // 2), pl.ds(BLK // 2, BLK // 2))

    def hcopy(d, backward, half):
        src = 0 if d == 0 else (2 * d if backward else 2 * d - 1)
        dst = 2 * d + 2 if backward else 2 * d + 1
        k = (4 if backward else 0) + d
        return rcopy(
            HALL.at[src, hv[half]], HALL.at[dst, hv[half]],
            h_s.at[1 if backward else 0], h_r.at[k, half], bwd if backward else fwd,
        )

    for half in (0, 1):
        hcopy(0, False, half).start()
        hcopy(0, True, half).start()

    tcopies[2].wait_recv()
    t_other.wait_recv()

    def stats(slot, blocks):
        n = len(blocks)
        hb = HALL[slot : slot + n].reshape(n * BLK, D)
        tg = [targets[pl.ds(dev(y, zz, c), 1), :] for zz in blocks]
        tg = tg[0] if n == 1 else jnp.concatenate(tg, 1)
        word = lax.broadcasted_iota(jnp.int32, (WORDS, n * BLK), 0)

        def body(k, carry):
            sums, picks = carry
            first = dev(k // 2, z, k % 2) * WORDS
            logits = lax.dot_general(
                T[k // 2, k % 2], hb, (((1,), (1,)), ((), ())), preferred_element_type=F32
            )
            sums = sums + jnp.sum(jnp.exp(logits), 0, keepdims=True)
            picks = picks + jnp.sum(jnp.where(word == tg - first, logits, 0.0), 0, keepdims=True)
            return sums, picks

        zero = jnp.zeros((1, n * BLK), F32)
        sums, picks = lax.fori_loop(0, 4, body, (zero, zero))
        for k, zz in enumerate(blocks):
            STL[pl.ds(zz, 1), :] = sums[:, k * BLK : (k + 1) * BLK]
            STL[pl.ds(NZ + zz, 1), :] = picks[:, k * BLK : (k + 1) * BLK]

    stats(0, [z])
    for d in (1, 2, 3, 4):
        for half in (0, 1):
            hcopy(d - 1, False, half).wait_recv()
            if d < 4:
                hcopy(d, False, half).start()
                hcopy(d - 1, True, half).wait_recv()
                if d < 3:
                    hcopy(d, True, half).start()
        if d < 4:
            stats(2 * d - 1, [zoff(-sgn * d), zoff(sgn * d)])
        else:
            stats(7, [zoff(4)])

    scopies = []
    for k in range(1, NZ):
        cp = rcopy(STL, ST.at[k], st_s.at[k - 1], st_r.at[k - 1], {"seq": dev(y, zoff(k), c)})
        cp.start()
        scopies.append(cp)
    ST[0] = STL[...]
    for cp in scopies:
        cp.wait_recv()

    def add(k, total):
        return total + ST[(z + 2 * NZ - k) % NZ]

    total = lax.fori_loop(0, NZ, add, jnp.zeros((2 * NZ, BLK), F32))
    token = lax.broadcasted_iota(jnp.int32, (NZ, BLK), 0) * (2 * BLK) + (
        lax.broadcasted_iota(jnp.int32, (NZ, BLK), 1) + (y * NZ * 2 + c) * BLK
    )
    per_token = jnp.where(token < vlen[0], jnp.log(total[:NZ]) - total[NZ:], 0.0)
    mine = lax.broadcasted_iota(jnp.int32, (NZ, BLK), 0) == z
    tl_out[...] = jnp.sum(jnp.where(mine, per_token, 0.0), 0, keepdims=True)
    PART[pl.ds(2 * y + c, 1)] = per_token[None]
    pc = []
    for k, to in enumerate((partner, near, diag)):
        s = PART.at[2 * y + c]
        cp = rcopy(s, s, p_s.at[k], p_r.at[k], to)
        cp.start()
        pc.append(cp)
    for cp in pc:
        cp.wait_recv()
    loss = jnp.sum(PART[0] + PART[1] + (PART[2] + PART[3])) / vlen[0].astype(F32)
    loss_out[...] = jnp.full((1, BLK), loss, F32)

    for cp in pc + scopies:
        cp.wait_send()
    drain(G0 + G1 + G2)
    halo0.wait_send()
    halo1.wait_send()
    for cp in tcopies + [t_other]:
        cp.wait_send()
    for k, n in ((0, 4), (1, 3)):
        s = HALL.at[pl.ds(0, n)]
        rcopy(s, s, h_s.at[k], h_r.at[0, 0], fwd).wait_send()


def on_device(
    embedded, w_qkv, w_out, w_pos, bias_content, bias_position, norm_gain, norm_offset,
    table, targets, valid_length,
):
    pos_share = jnp.einsum(
        "ldc,dm->lcm", w_pos, pos_table_t(2 * BLK, D), preferred_element_type=F32
    ).astype(BF)
    po_in = jnp.concatenate([pos_share, w_out], 2)
    vmem = pl.BlockSpec(memory_space=pltpu.VMEM)
    hbm = pl.BlockSpec(memory_space=pl.ANY)
    smem = pl.BlockSpec(memory_space=pltpu.SMEM)
    DMA = pltpu.SemaphoreType.DMA
    hidden, token_loss, loss = pl.pallas_call(
        kernel,
        out_shape=(
            jax.ShapeDtypeStruct((BLK, D), BF),
            jax.ShapeDtypeStruct((1, BLK), F32),
            jax.ShapeDtypeStruct((1, BLK), F32),
        ),
        in_specs=[hbm, hbm, hbm, vmem, vmem, vmem, vmem, hbm, vmem, smem],
        out_specs=(vmem, vmem, vmem),
        scratch_shapes=[
            pltpu.VMEM((LAYERS, 2, NZ, 2, SHARD, 3 * D), BF),
            pltpu.VMEM((LAYERS, 2, NZ, 2, SHARD, PO), BF),
            pltpu.VMEM((2, 2, WORDS, D), BF),
            pltpu.VMEM((2, BLK, D), BF),
            pltpu.VMEM((2, BLK, D), BF),
            pltpu.VMEM((BLK, D), BF),
            pltpu.VMEM((BLK, D), BF),
            pltpu.VMEM((2 * BLK, D), BF),
            pltpu.VMEM((2 * BLK, D), BF),
            pltpu.VMEM((BLK, D), BF),
            pltpu.VMEM((BLK, D), F32),
            pltpu.VMEM((NZ, BLK, D), BF),
            pltpu.VMEM((2 * NZ, BLK), F32),
            pltpu.VMEM((NZ, 2 * NZ, BLK), F32),
            pltpu.VMEM((4, NZ, BLK), F32),
            DMA((5,)),
            DMA((8, 7)),
            DMA((8, 2)),
            DMA((8, 2)),
            DMA((8, 6)),
            DMA((2,)),
            DMA((2,)),
            DMA((4,)),
            DMA((4,)),
            DMA((2,)),
            DMA((7, 2)),
            DMA((NZ - 1,)),
            DMA((NZ - 1,)),
            DMA((3,)),
            DMA((3,)),
        ],
        compiler_params=pltpu.CompilerParams(
            collective_id=0, has_side_effects=True, vmem_limit_bytes=58 * 1024 * 1024
        ),
    )(
        embedded, w_qkv, po_in, bias_content, bias_position, norm_gain, norm_offset,
        table, targets.reshape(32, BLK), valid_length,
    )
    return hidden, token_loss.reshape(BLK), loss[0, :1]


def solution(mesh):
    in_specs = (
        P(("batch", "seq"), None),
        P(None, "seq", None),
        P(None, "seq", None),
        P(None, None, "seq"),
        P(),
        P(),
        P(),
        P(),
        P("seq", None),
        P("batch"),
        P("batch"),
    )
    out_specs = (P(("batch", "seq"), None), P(("batch", "seq")), P("batch"))
    return jax.shard_map(
        on_device, mesh=mesh, in_specs=in_specs, out_specs=out_specs, check_vma=False
    )
```

time: 380 us -> 126 us (0.33)
  waiting for transfers between devices: 216 us -> 0 us
  Pallas kernels: 0 us -> 118 us
  starting transfers between devices: 51.3 us -> 0 us
  matrix products: 41.5 us -> 1.28 us
  local copies, waits for them, and re-layouts: 38.2 us -> 2.52 us
  other arithmetic: 15.1 us -> 0.68 us
  between operations: 16.8 us -> 2.53 us
    pallas_call x0 -> x1, Pallas kernels: none -> 118 us  [on_device(): pl.pallas_call(kernel, out_shape=(jax.ShapeDtypeStruct((BLK, D), BF), jax...]
    all_gather x3 -> x0, waiting for transfers between devices: 114 us -> none  [the longest x1 73.4 us: on_device(): lax.all_gather(hidden, 'seq', axis=0, tiled=True)]
    all_to_all x6 -> x0, waiting for transfers between devices: 61.5 us -> none  [copy_for_each(): lax.all_to_all(jnp.broadcast_to(x[None], (devices, *x.shape)), axis, 0, 0...]
    all_to_all x6 -> x0, starting transfers between devices: 42.7 us -> none  [copy_for_each(): lax.all_to_all(jnp.broadcast_to(x[None], (devices, *x.shape)), axis, 0, 0...]
    dot_general x15 -> x0, matrix products: 41.5 us -> none  [the longest x1 9.82 us: on_device(): jnp.einsum('td,vd->tv', lax.all_gather(hidden, 'seq', axis=0, tiled=True)...]
    ppermute x2 -> x0, waiting for transfers between devices: 40 us -> none  [passed_along(): return lax.ppermute(x, axis, pairs)]
    ppermute x2 -> x0, starting transfers between devices: 8.45 us -> none  [passed_along(): return lax.ppermute(x, axis, pairs)]
    concatenate x4 -> x0, local copies, waits for them, and re-layouts: 7.44 us -> none  [the longest x2 4.15 us: attention_layer(): jnp.concatenate([memory_values, value_rows], 0)]
  transfers between devices with their start and end apart: 11 -> 0, of which waited for: 9 -> 0; matrix products, arithmetic and copies ran while one was open for 19% -> 0% of each run, Pallas kernels for 0% -> 0%
where the time goes in v1:
time: 126 us; the launch traced here: 125 us
  Pallas kernels  118 us (94%)
  between operations  2.53 us (2%)
  local copies, waits for them, and re-layouts  2.52 us (2%)
  matrix products  1.28 us (1%)
    pallas_call x1, Pallas kernels, on_device(): pl.pallas_call(kernel, out_shape=(jax.ShapeDtypeStruct((BLK, D), BF), jax...  118 us
    unnamed x10, local copies, waits for them, and re-layouts  2.52 us

profile of v1, /device:TPU:1, one launch (start us, length us, event | category | flops | bytes accessed | tf_op | source)
XLA Modules:
  0.0 125.5 jit_solution(15214165599328168488)
XLA Ops:
  0.6 0.0 copy-start
  1.3 0.2 copy-done
  1.6 0.0 copy-start.1
  1.6 1.3 %fusion = f32[256,64]{0,1:S(1)} fusion(bf16[1024,64]{0,1:T(8,128)(2,1)S(1)} %bitcast.12, bf16[1024,256]{1,0:T(8,128)(2,1)} %constant.5), kind=kOutput, calls=%fused_computation.2 | convolution fusion | flops 33554432 | bytes 720896
  2.9 0.0 copy-done.1
  2.9 0.7 pad_maximum_fusion.po_in
  3.6 118.5 %shard_map.139 = (bf16[128,1024]{1,0:T(8,128)(2,1)}, f32[1,128]{1,0:T(1,128)}, f32[1,128]{1,0:T(1,128)}) custom-call(bf16[128,1024]{1,0:T(8,128)(2,1)} %emb.1, bf16[2,32,3072]{2,1,0:T(8,128)(2,1)} %wqkv.1, bf16[2,32,1280]{2,1,0:T(8,128)(2,1)} %pad_maximum_fusion.po_in, f32[2,1024]{1,0:T(2,128)} %bias_c.1, f32[2,1024]{1,0:T(2,128)} %bias_p.1, ...), custom_call_target="tpu_custom_call" | custom-call | tf_op jit(solution)/shard_map/pallas_call | solution.py:397
  122.0 0.0 copy-start.3
  122.0 1.7 %copy.19 = bf16[128,1024]{1,0:T(8,128)(2,1)} copy(bf16[128,1024]{1,0:T(8,128)(2,1)} %get-tuple-element.12) | data formatting | bytes 524288
  123.7 0.0 copy-done.3
  123.7 0.0 copy-start.2
  123.7 0.5 copy.20
  124.2 0.1 copy-done.2
  (1 shorter events, 0.0 us)
Async XLA Ops:
  0.6 0.9 copy-start
  1.6 1.3 %copy-start.1 = (bf16[2,32,1024]{2,1,0:T(8,128)(2,1)S(1)}, bf16[2,32,1024]{2,1,0:T(8,128)(2,1)}, u32[]{:S(2)}) copy-start(bf16[2,32,1024]{2,1,0:T(8,128)(2,1)} %param.14) | copy-start | bytes 393220
  122.0 1.7 %copy-start.3 = (f32[1,128]{1,0:T(1,128)S(1)}, f32[1,128]{1,0:T(1,128)}, u32[]{:S(2)}) copy-start(f32[1,128]{1,0:T(1,128)} %get-tuple-element.7) | copy-start | bytes 1540
  123.7 0.6 copy-start.2

commit v2 on v1

--- a/solution.py
+++ b/solution.py
@@ -22,6 +22,28 @@
 F32 = jnp.float32
 
 
+ORDER = (
+    ("o", 0), ("o", 1), ("f", 0, 1), ("b", 0, 1), ("y", 0, 0), ("o", 2), ("f", 1, 1),
+    ("b", 1, 1), ("f", 0, 2), ("y", 0, 4), ("b", 0, 2), ("y", 0, 1), ("f", 2, 1), ("b", 2, 1),
+    ("y", 2, 0), ("f", 1, 2), ("b", 1, 2), ("y", 0, 5), ("f", 0, 3), ("b", 0, 3), ("y", 0, 2),
+    ("y", 2, 4), ("f", 2, 2), ("o", 3), ("b", 2, 2), ("y", 2, 1), ("o", 4), ("f", 1, 3),
+    ("b", 1, 3), ("f", 0, 4), ("d", 0, 0), ("y", 0, 6), ("y", 0, 3), ("f", 2, 3), ("y", 2, 5),
+    ("b", 3, 1), ("y", 3, 0), ("f", 3, 1), ("o", 5), ("b", 2, 3), ("y", 2, 2), ("d", 0, 2),
+    ("f", 4, 1), ("b", 4, 1), ("y", 0, 7), ("d", 0, 1), ("f", 1, 4), ("d", 1, 0), ("y", 2, 6),
+    ("b", 3, 2), ("f", 2, 4), ("d", 2, 0), ("b", 5, 1), ("y", 3, 4), ("y", 3, 1), ("f", 3, 2),
+    ("b", 4, 2), ("y", 5, 0), ("d", 0, 3), ("f", 5, 1), ("b", 3, 3), ("d", 1, 1), ("y", 2, 3),
+    ("d", 2, 2), ("f", 4, 2), ("b", 5, 2), ("y", 2, 7), ("d", 2, 1), ("f", 3, 3), ("b", 4, 3),
+    ("y", 3, 5), ("c", "q0"), ("y", 3, 2), ("f", 5, 2), ("c", "v0"), ("d", 2, 3), ("f", 4, 3),
+    ("b", 5, 3), ("y", 5, 1), ("y", 5, 4), ("f", 3, 4), ("d", 3, 0), ("f", 5, 3), ("y", 3, 6),
+    ("c", "a00"), ("y", 3, 3), ("c", "a01"), ("f", 4, 4), ("d", 4, 0), ("y", 5, 2),
+    ("y", 5, 5), ("c", "a02"), ("c", "a03"), ("f", 5, 4), ("d", 5, 0), ("t", 0), ("c", "p0"),
+    ("y", 3, 7), ("d", 3, 2), ("d", 3, 1), ("y", 5, 3), ("c", "n0"), ("y", 5, 6), ("d", 5, 2),
+    ("d", 4, 1), ("y", 5, 7), ("d", 5, 1), ("d", 3, 3), ("d", 5, 3), ("c", "q1"), ("c", "k1"),
+    ("c", "m1"), ("c", "a10"), ("c", "a11"), ("c", "a12"), ("c", "a13"), ("c", "p1"), ("t", 1),
+    ("c", "n1"),
+)
+
+
 def pos_table_t(row_count, model_width):
     distance = np.arange(row_count - 1, -1, -1).astype(np.float32)
     inverse = np.float32(1.0) / np.float32(10000.0) ** (
@@ -33,10 +55,10 @@
 
 
 def kernel(
-    emb, wqkv, po_in, bias_c, bias_p, gain, offset, table, targets, vlen,
+    emb, wqkv, w_out, w_pos, ptab, bias_c, bias_p, gain, offset, table, targets, vlen,
     hid_out, tl_out, loss_out,
-    W, POW, T, X0, X1, QC, QP, K, V, ATT, Y, HALL, STL, ST, PART,
-    lsem, ring_r, y_r, d_r, w_s, halo_s, halo_r, t_s, t_r, h_s, h_r, st_s, st_r, p_s, p_r,
+    W, POW, T, X0, X1, QC, QP, K, V, ATT, Y, HALL, STL, ST, PART, WP, PT,
+    lsem, ring_r, y_r, x_r, d_r, w_s, halo_s, halo_r, t_s, t_r, h_s, h_r, st_s, st_r, p_s, p_r,
 ):
     i = lax.axis_index("seq")
     b = lax.axis_index("batch")
@@ -59,6 +81,10 @@
     far = {"seq": dev(1 - y, z, c), "batch": (b // 2) * 2 + 1 - b % 2}
     nxt = {"seq": (i + 1) % 32}
     prv = {"seq": (i + 31) % 32}
+    x = b // 2
+    xp = x % 2
+    right = {"batch": ((x + 1) % 4) * 2 + b % 2}
+    left = {"batch": ((x + 3) % 4) * 2 + b % 2}
 
     def rcopy(src, dst, ss, rs, to):
         return pltpu.make_async_remote_copy(
@@ -68,9 +94,11 @@
     loc = [
         pltpu.make_async_copy(wqkv.at[0], W.at[0, y, z, c], lsem.at[0]),
         pltpu.make_async_copy(emb, X0.at[1], lsem.at[1]),
-        pltpu.make_async_copy(po_in, POW.at[:, y, z, c], lsem.at[2]),
-        pltpu.make_async_copy(wqkv.at[1], W.at[1, y, z, c], lsem.at[3]),
-        pltpu.make_async_copy(table, T.at[y, c], lsem.at[4]),
+        pltpu.make_async_copy(w_pos, WP, lsem.at[2]),
+        pltpu.make_async_copy(ptab, PT, lsem.at[3]),
+        pltpu.make_async_copy(w_out, POW.at[:, y, z, c, :, pl.ds(256, D)], lsem.at[4]),
+        pltpu.make_async_copy(wqkv.at[1], W.at[1, y, z, c], lsem.at[5]),
+        pltpu.make_async_copy(table, T.at[y, c], lsem.at[6]),
     ]
     for cp in loc:
         cp.start()
@@ -78,61 +106,94 @@
     barrier = pltpu.get_barrier_semaphore()
     for k in range(1, NZ):
         pl.semaphore_signal(barrier, inc=1, device_id={"seq": dev(y, zoff(k), c)}, device_id_type=MESH)
-    for peer in (partner, diag, near, far, nxt, prv):
+    for peer in (partner, diag, near, far, nxt, prv, right, left):
         pl.semaphore_signal(barrier, inc=1, device_id=peer, device_id_type=MESH)
-    pl.semaphore_wait(barrier, NZ - 1 + 6)
-
-    def stream(si, yy, zz):
-        if si in (3, 7):
-            return POW.at[si // 4, yy, zz, c]
-        layer, col = (0, si) if si < 3 else (1, si - 4)
-        return W.at[layer, yy, zz, c, :, pl.ds(col * D, D)]
-
-    def own(group):
-        for si in group:
-            s = stream(si, y, z)
-            rcopy(s, s, w_s.at[si, 0], ring_r.at[si, 0], fwd).start()
-            rcopy(s, s, w_s.at[si, 1], ring_r.at[si, 4], bwd).start()
-            rcopy(s, s, w_s.at[si, 2], y_r.at[si, 0], near).start()
-
-    def step(group, d):
-        for si in group:
-            s = stream(si, y, zoff(-sgn * d))
-            rcopy(s, s, w_s.at[si, 0], ring_r.at[si, d - 1], fwd).wait_recv()
-            if d < 4:
-                rcopy(s, s, w_s.at[si, 0], ring_r.at[si, d], fwd).start()
-            rcopy(s, s, w_s.at[si, 3], y_r.at[si, 1], far).start()
-            if d < 4:
-                s = stream(si, y, zoff(sgn * d))
-                rcopy(s, s, w_s.at[si, 1], ring_r.at[si, 3 + d], bwd).wait_recv()
-                if d < 3:
-                    rcopy(s, s, w_s.at[si, 1], ring_r.at[si, 4 + d], bwd).start()
-                rcopy(s, s, w_s.at[si, 2], y_r.at[si, 0], near).start()
-
-    def d2d_own(group):
-        for si in group:
-            s = stream(si, y, pl.ds(0, NZ))
-            rcopy(s, s, w_s.at[si, 4], d_r.at[si, 0], partner).start()
-
-    def d2d_other(group):
-        for si in group:
-            s4 = stream(si, 1 - y, pl.ds(0, 4))
-            rcopy(s4, s4, w_s.at[si, 2], y_r.at[si, 0], near).wait_recv()
-            rcopy(s4, s4, w_s.at[si, 3], y_r.at[si, 1], far).wait_recv()
-            s = stream(si, 1 - y, pl.ds(0, NZ))
-            rcopy(s, s, w_s.at[si, 5], d_r.at[si, 1], partner).start()
-
-    def finish(group):
-        for si in group:
-            s = stream(si, y, pl.ds(0, NZ))
-            rcopy(s, s, w_s.at[si, 4], d_r.at[si, 0], partner).wait_recv()
-            rcopy(s, s, w_s.at[si, 5], d_r.at[si, 1], partner).wait_recv()
-
-    def drain(group):
-        for si in group:
-            for k, n in ((0, 4), (1, 3), (2, 4), (3, 4), (4, 8), (5, 8)):
-                s = stream(si, y, pl.ds(0, n))
-                rcopy(s, s, w_s.at[si, k], ring_r.at[si, 0], fwd).wait_send()
+    pl.semaphore_wait(barrier, NZ - 1 + 8)
+
+    def piece(si, yy, zz, kind):
+        layer, part = si // 3, si % 3
+        if part == 2:
+            at, size = {"ring": (xp * 384, 896), "give": (xp * 896, 384), "take": ((1 - xp) * 896, 384)}[kind]
+            return POW.at[layer, yy, zz, c, :, pl.ds(pl.multiple_of(at, 128), size)]
+        if part == 1:
+            return W.at[layer, yy, zz, c, :, pl.ds(D, D)]
+        at = (1 - xp if kind == "take" else xp) * 2 * D
+        return W.at[layer, yy, zz, c, :, pl.ds(pl.multiple_of(at, D), D)]
+
+    def shares(si):
+        return si % 3 != 1
+
+    def place(k):
+        return zoff(sgn * k) if k < 4 else zoff(-sgn * (k - 3))
+
+    def ring_copy(si, zz, to, k):
+        s = piece(si, y, zz, "ring")
+        return rcopy(s, s, w_s.at[si, 0 if k < 4 else 1], ring_r.at[si, k], to)
+
+    def y_copy(si, k):
+        s = piece(si, y, place(k), "ring")
+        slot = k if shares(si) else k // 4 * 4
+        return rcopy(s, s, w_s.at[si, 2 + k // 4], y_r.at[si, slot], far if k >= 4 else near)
+
+    def x_copy(si, yy, k, other):
+        s = piece(si, yy, place(k), "give")
+        return rcopy(s, s, w_s.at[si, 4 + k // 4], x_r.at[si, 2 * other + k // 4], left if k >= 4 else right)
+
+    def d_copy(si, n):
+        s = piece(si, y if n % 2 == 0 else 1 - y, pl.ds(0, NZ), "ring" if n < 2 else "take")
+        return rcopy(s, s, w_s.at[si, 6 + n], d_r.at[si, n], partner)
+
+    def several(si, kind, recv, n=4):
+        s = piece(si, y, pl.ds(0, n), kind)
+        return rcopy(s, s, w_s.at[si, 0], recv, partner)
+
+    def own(si):
+        ring_copy(si, z, fwd, 0).start()
+        ring_copy(si, z, bwd, 4).start()
+        y_copy(si, 0).start()
+
+    def forward(si, d):
+        zz = zoff(-sgn * d)
+        ring_copy(si, zz, fwd, d - 1).wait_recv()
+        if d < 4:
+            ring_copy(si, zz, fwd, d).start()
+        y_copy(si, 3 + d).start()
+        if shares(si):
+            x_copy(si, y, 3 + d, 0).start()
+
+    def backward(si, d):
+        zz = zoff(sgn * d)
+        ring_copy(si, zz, bwd, 3 + d).wait_recv()
+        if d < 3:
+            ring_copy(si, zz, bwd, 4 + d).start()
+        y_copy(si, d).start()
+        if shares(si):
+            x_copy(si, y, d, 0).start()
+
+    def across(si, k):
+        y_copy(si, k).wait_recv()
+        x_copy(si, 1 - y, k, 1).start()
+
+    def to_partner(si, n):
+        if n == 1 and not shares(si):
+            several(si, "ring", y_r.at[si, 0]).wait_recv()
+            several(si, "ring", y_r.at[si, 4]).wait_recv()
+        if n >= 2:
+            several(si, "take", x_r.at[si, 2 * n - 4], n + 1).wait_recv()
+            several(si, "take", x_r.at[si, 2 * n - 3]).wait_recv()
+        d_copy(si, n).start()
+
+    def finish(si):
+        for n in range(4 if shares(si) else 2):
+            d_copy(si, n).wait_recv()
+
+    def drain(si):
+        waits = [("ring", 0, 4), ("ring", 1, 3), ("ring", 2, 4), ("ring", 3, 4), ("ring", 6, 8), ("ring", 7, 8)]
+        if shares(si):
+            waits += [("give", 4, 7), ("give", 5, 8), ("take", 8, 8), ("take", 9, 8)]
+        for kind, k, n in waits:
+            s = piece(si, y, pl.ds(0, n), kind)
+            rcopy(s, s, w_s.at[si, k], ring_r.at[si, 0], fwd).wait_send()
 
     low = lax.broadcasted_iota(jnp.int32, (BLK, BLK), 1) < 64
     rows = lax.broadcasted_iota(jnp.int32, (BLK, 2 * BLK), 0)
@@ -220,69 +281,78 @@
 
         lax.fori_loop(0, 4, body, 0)
 
-    G0, G1, G2 = (0, 1, 2), (3, 4), (5, 6, 7)
-
-    loc[0].wait()
-    own(G0)
-    loc[1].wait()
-    halo0 = rcopy(X0.at[1], X0.at[0], halo_s.at[0], halo_r.at[0], nxt)
-    halo0.start()
-    for cp in loc[2:]:
-        cp.wait()
-    for d in (1, 2, 3):
-        step(G0, d)
-    own(G1)
-    step(G0, 4)
-    d2d_own(G0)
-    step(G1, 1)
-    d2d_other(G0)
     halves = (pl.ds(0, WORDS // 2), pl.ds(WORDS // 2, WORDS // 2))
     tcopies = [
         rcopy(T.at[y, c, h], T.at[y, c, h], t_s.at[k], t_r.at[k], to)
         for k, (h, to) in enumerate(zip(halves, (near, far)))
     ] + [rcopy(T.at[y, c], T.at[y, c], t_s.at[2], t_r.at[2], partner)]
-    tcopies[2].start()
-    finish(G0)
-    halo0.wait_recv()
-    queries(0, X0)
-    step(G1, 2)
-    keys_values(0, X0, "all")
-    step(G1, 3)
-    own(G2)
-    step(G1, 4)
-    d2d_own(G1)
-    d2d_other(G1[:1])
-    finish(G1[:1])
-    attend(0, 0, 3)
-    step(G2, 1)
-    attend(0, 3, 6)
-    d2d_other(G1[1:])
-    attend(0, 6, 8)
-    step(G2, 2)
-    project(0, X0)
-    norm(0, X1.at[1], False)
+    t_other = rcopy(T.at[1 - y, c], T.at[1 - y, c], t_s.at[3], t_r.at[3], partner)
+    halo0 = rcopy(X0.at[1], X0.at[0], halo_s.at[0], halo_r.at[0], nxt)
     halo1 = rcopy(X1.at[1], X1.at[0], halo_s.at[1], halo_r.at[1], nxt)
-    halo1.start()
-    finish(G1[1:])
-    queries(1, X1)
-    step(G2, 3)
-    step(G2, 4)
-    d2d_own(G2)
-    tcopies[0].start()
-    tcopies[1].start()
-    d2d_other(G2)
-    finish(G2[:2])
-    keys_values(1, X1, "own")
-    halo1.wait_recv()
-    keys_values(1, X1, "memory")
-    finish(G2[2:])
-    attend(1, 0, 8)
-    tcopies[0].wait_recv()
-    tcopies[1].wait_recv()
-    t_other = rcopy(T.at[1 - y, c], T.at[1 - y, c], t_s.at[3], t_r.at[3], partner)
-    t_other.start()
-    project(1, X1)
-    norm(1, HALL.at[0], True)
+
+    def table_step(n):
+        if n == 0:
+            for cp in tcopies:
+                cp.start()
+        else:
+            tcopies[0].wait_recv()
+            tcopies[1].wait_recv()
+            t_other.start()
+
+    def compute(name):
+        kind, layer = name[0], int(name[1])
+        X = (X0, X1)[layer]
+        if name == "q0":
+            finish(0)
+            finish(1)
+            queries(0, X0)
+        elif name == "v0":
+            halo0.wait_recv()
+            keys_values(0, X0, "all")
+        elif name == "q1":
+            finish(3)
+            finish(4)
+            queries(1, X1)
+        elif name == "k1":
+            keys_values(1, X1, "own")
+        elif name == "m1":
+            halo1.wait_recv()
+            keys_values(1, X1, "memory")
+        elif kind == "a":
+            k = int(name[2])
+            if k == 0:
+                finish(2 + 3 * layer)
+            attend(layer, 2 * k, 2 * k + 2)
+        elif kind == "p":
+            project(layer, X)
+        elif name == "n0":
+            norm(0, X1.at[1], False)
+            halo1.start()
+        else:
+            norm(1, HALL.at[0], True)
+
+    def start_rest():
+        loc[1].wait()
+        halo0.start()
+        loc[2].wait()
+        loc[3].wait()
+        for layer in range(LAYERS):
+            share = lax.dot_general(
+                WP[layer], PT[...], (((0,), (0,)), ((), ())), preferred_element_type=F32
+            )
+            POW[layer, y, z, c, :, 0:256] = share.astype(BF)
+        for cp in loc[4:]:
+            cp.wait()
+
+    handlers = {"o": own, "f": forward, "b": backward, "y": across, "d": to_partner, "t": table_step}
+    loc[0].wait()
+    for n, (kind, *at) in enumerate(ORDER):
+        if kind == "c":
+            compute(at[0])
+        else:
+            handlers[kind](*at)
+        if n == 1:
+            start_rest()
 
     hv = (pl.ds(0, BLK // 2), pl.ds(BLK // 2, BLK // 2))
 
@@ -372,7 +442,8 @@
 
     for cp in pc + scopies:
         cp.wait_send()
-    drain(G0 + G1 + G2)
+    for si in range(6):
+        drain(si)
     halo0.wait_send()
     halo1.wait_send()
     for cp in tcopies + [t_other]:
@@ -386,10 +457,6 @@
     embedded, w_qkv, w_out, w_pos, bias_content, bias_position, norm_gain, norm_offset,
     table, targets, valid_length,
 ):
-    pos_share = jnp.einsum(
-        "ldc,dm->lcm", w_pos, pos_table_t(2 * BLK, D), preferred_element_type=F32
-    ).astype(BF)
-    po_in = jnp.concatenate([pos_share, w_out], 2)
     vmem = pl.BlockSpec(memory_space=pltpu.VMEM)
     hbm = pl.BlockSpec(memory_space=pl.ANY)
     smem = pl.BlockSpec(memory_space=pltpu.SMEM)
@@ -401,7 +468,7 @@
             jax.ShapeDtypeStruct((1, BLK), F32),
             jax.ShapeDtypeStruct((1, BLK), F32),
         ),
-        in_specs=[hbm, hbm, hbm, vmem, vmem, vmem, vmem, hbm, vmem, smem],
+        in_specs=[hbm] * 5 + [vmem] * 4 + [hbm, vmem, smem],
         out_specs=(vmem, vmem, vmem),
         scratch_shapes=[
             pltpu.VMEM((LAYERS, 2, NZ, 2, SHARD, 3 * D), BF),
@@ -419,11 +486,14 @@
             pltpu.VMEM((2 * NZ, BLK), F32),
             pltpu.VMEM((NZ, 2 * NZ, BLK), F32),
             pltpu.VMEM((4, NZ, BLK), F32),
-            DMA((5,)),
-            DMA((8, 7)),
-            DMA((8, 2)),
-            DMA((8, 2)),
-            DMA((8, 6)),
+            pltpu.VMEM((LAYERS, D, SHARD), BF),
+            pltpu.VMEM((D, 2 * BLK), BF),
+            DMA((7,)),
+            DMA((6, 7)),
+            DMA((6, 8)),
+            DMA((6, 4)),
+            DMA((6, 4)),
+            DMA((6, 10)),
             DMA((2,)),
             DMA((2,)),
             DMA((4,)),
@@ -439,7 +509,7 @@
             collective_id=0, has_side_effects=True, vmem_limit_bytes=58 * 1024 * 1024
         ),
     )(
-        embedded, w_qkv, po_in, bias_content, bias_position, norm_gain, norm_offset,
+        embedded, w_qkv, w_out, w_pos, pos_table_t(2 * BLK, D), bias_content, bias_position, norm_gain, norm_offset,
         table, targets.reshape(32, BLK), valid_length,
     )
     return hidden, token_loss.reshape(BLK), loss[0, :1]

time: 126 us -> 108 us (0.86)
  Pallas kernels: 118 us -> 101 us
  local copies, waits for them, and re-layouts: 2.52 us -> 4.2 us
  matrix products: 1.28 us -> 0 us
    pallas_call x1, Pallas kernels: 118 us -> 101 us  [on_device(): pl.pallas_call(kernel, out_shape=(jax.ShapeDtypeStruct((BLK, D), BF), jax...]
    unnamed x10 -> x7, local copies, waits for them, and re-layouts: 2.52 us -> 4.2 us
    unnamed x1 -> x0, matrix products: 1.28 us -> none
where the time goes in v2:
time: 108 us
  Pallas kernels  101 us (94%)
  local copies, waits for them, and re-layouts  4.2 us (4%)
  between operations  2.46 us (2%)
    pallas_call x1, Pallas kernels, on_device(): pl.pallas_call(kernel, out_shape=(jax.ShapeDtypeStruct((BLK, D), BF), jax...  101 us
    unnamed x7, local copies, waits for them, and re-layouts  4.2 us

profile of v2, /device:TPU:1, one launch (start us, length us, event | category | flops | bytes accessed | tf_op | source)
XLA Modules:
  0.0 108.1 jit_solution(10482585398439803820)
XLA Ops:
  1.3 1.9 %copy.15.w_pos = bf16[2,1024,32]{2,1,0:T(8,128)(2,1)} copy(bf16[2,1024,32]{1,2,0:T(8,128)(2,1)} %param.15) | data formatting | bytes 262144 | tf_op args[3]
  3.2 101.4 %shard_map.139 = (bf16[128,1024]{1,0:T(8,128)(2,1)}, f32[1,128]{1,0:T(1,128)}, f32[1,128]{1,0:T(1,128)}) custom-call(bf16[128,1024]{1,0:T(8,128)(2,1)} %emb.1, bf16[2,32,3072]{2,1,0:T(8,128)(2,1)} %wqkv.1, bf16[2,32,1024]{2,1,0:T(8,128)(2,1)} %w_out.1, bf16[2,1024,32]{2,1,0:T(8,128)(2,1)} %copy.15.w_pos, bf16[1024,256]{1,0:T(8,128)(2,1)} %constant.5.ptab, ...), custom_call_target="tpu_custom_call" | custom-call | tf_op jit(solution)/shard_map/pallas_call | solution.py:464
  104.6 0.0 copy-start.1
  104.6 1.7 %copy.20 = bf16[128,1024]{1,0:T(8,128)(2,1)} copy(bf16[128,1024]{1,0:T(8,128)(2,1)} %get-tuple-element.12) | data formatting | bytes 524288
  106.3 0.0 copy-done.1
  106.3 0.0 copy-start
  106.3 0.5 copy.21
  106.8 0.1 copy-done
Async XLA Ops:
  104.6 1.7 %copy-start.1 = (f32[1,128]{1,0:T(1,128)S(1)}, f32[1,128]{1,0:T(1,128)}, u32[]{:S(2)}) copy-start(f32[1,128]{1,0:T(1,128)} %get-tuple-element.7) | copy-start | bytes 1540
  106.3 0.6 copy-start

commit v3 on v2

--- a/solution.py
+++ b/solution.py
@@ -23,24 +23,24 @@
 
 
 ORDER = (
-    ("o", 0), ("o", 1), ("f", 0, 1), ("b", 0, 1), ("y", 0, 0), ("o", 2), ("f", 1, 1),
-    ("b", 1, 1), ("f", 0, 2), ("y", 0, 4), ("b", 0, 2), ("y", 0, 1), ("f", 2, 1), ("b", 2, 1),
-    ("y", 2, 0), ("f", 1, 2), ("b", 1, 2), ("y", 0, 5), ("f", 0, 3), ("b", 0, 3), ("y", 0, 2),
-    ("y", 2, 4), ("f", 2, 2), ("o", 3), ("b", 2, 2), ("y", 2, 1), ("o", 4), ("f", 1, 3),
-    ("b", 1, 3), ("f", 0, 4), ("d", 0, 0), ("y", 0, 6), ("y", 0, 3), ("f", 2, 3), ("y", 2, 5),
-    ("b", 3, 1), ("y", 3, 0), ("f", 3, 1), ("o", 5), ("b", 2, 3), ("y", 2, 2), ("d", 0, 2),
-    ("f", 4, 1), ("b", 4, 1), ("y", 0, 7), ("d", 0, 1), ("f", 1, 4), ("d", 1, 0), ("y", 2, 6),
-    ("b", 3, 2), ("f", 2, 4), ("d", 2, 0), ("b", 5, 1), ("y", 3, 4), ("y", 3, 1), ("f", 3, 2),
-    ("b", 4, 2), ("y", 5, 0), ("d", 0, 3), ("f", 5, 1), ("b", 3, 3), ("d", 1, 1), ("y", 2, 3),
-    ("d", 2, 2), ("f", 4, 2), ("b", 5, 2), ("y", 2, 7), ("d", 2, 1), ("f", 3, 3), ("b", 4, 3),
-    ("y", 3, 5), ("c", "q0"), ("y", 3, 2), ("f", 5, 2), ("c", "v0"), ("d", 2, 3), ("f", 4, 3),
-    ("b", 5, 3), ("y", 5, 1), ("y", 5, 4), ("f", 3, 4), ("d", 3, 0), ("f", 5, 3), ("y", 3, 6),
-    ("c", "a00"), ("y", 3, 3), ("c", "a01"), ("f", 4, 4), ("d", 4, 0), ("y", 5, 2),
-    ("y", 5, 5), ("c", "a02"), ("c", "a03"), ("f", 5, 4), ("d", 5, 0), ("t", 0), ("c", "p0"),
-    ("y", 3, 7), ("d", 3, 2), ("d", 3, 1), ("y", 5, 3), ("c", "n0"), ("y", 5, 6), ("d", 5, 2),
-    ("d", 4, 1), ("y", 5, 7), ("d", 5, 1), ("d", 3, 3), ("d", 5, 3), ("c", "q1"), ("c", "k1"),
-    ("c", "m1"), ("c", "a10"), ("c", "a11"), ("c", "a12"), ("c", "a13"), ("c", "p1"), ("t", 1),
-    ("c", "n1"),
+    ("o", 0), ("o", 1), ("o", 2), ("f", 0, 1), ("b", 0, 1), ("y", 0, 0), ("f", 1, 1),
+    ("b", 1, 1), ("f", 2, 1), ("b", 2, 1), ("y", 2, 0), ("y", 0, 4), ("f", 0, 2), ("b", 0, 2),
+    ("y", 0, 1), ("f", 1, 2), ("b", 1, 2), ("y", 2, 4), ("f", 2, 2), ("b", 2, 2), ("y", 2, 1),
+    ("y", 0, 5), ("f", 0, 3), ("b", 0, 3), ("y", 0, 2), ("o", 3), ("f", 1, 3), ("b", 1, 3),
+    ("y", 2, 5), ("f", 2, 3), ("b", 2, 3), ("y", 2, 2), ("y", 0, 6), ("f", 0, 4), ("y", 0, 3),
+    ("d", 0, 0), ("b", 3, 1), ("f", 3, 1), ("o", 4), ("o", 5), ("f", 1, 4), ("d", 1, 0),
+    ("y", 3, 0), ("f", 2, 4), ("d", 2, 0), ("y", 2, 6), ("b", 3, 2), ("y", 0, 7), ("d", 0, 1),
+    ("y", 2, 3), ("f", 3, 2), ("b", 4, 1), ("d", 0, 2), ("y", 3, 4), ("y", 3, 1), ("b", 5, 1),
+    ("f", 4, 1), ("d", 1, 1), ("d", 2, 2), ("f", 5, 1), ("b", 3, 3), ("y", 2, 7), ("d", 2, 1),
+    ("y", 5, 0), ("f", 3, 3), ("d", 0, 3), ("b", 4, 2), ("y", 3, 5), ("y", 3, 2), ("b", 5, 2),
+    ("f", 4, 2), ("f", 5, 2), ("c", "q0"), ("c", "v0"), ("f", 3, 4), ("d", 3, 0), ("d", 2, 3),
+    ("b", 4, 3), ("y", 5, 1), ("y", 5, 4), ("y", 3, 6), ("b", 5, 3), ("f", 4, 3), ("y", 3, 3),
+    ("f", 5, 3), ("c", "a00"), ("c", "a01"), ("y", 5, 5), ("c", "a02"), ("f", 4, 4),
+    ("d", 4, 0), ("y", 5, 2), ("c", "a03"), ("y", 3, 7), ("d", 3, 2), ("d", 3, 1), ("f", 5, 4),
+    ("d", 5, 0), ("t", 0), ("c", "p0"), ("c", "n0"), ("y", 5, 3), ("y", 5, 6), ("d", 4, 1),
+    ("d", 3, 3), ("d", 5, 2), ("y", 5, 7), ("d", 5, 1), ("c", "q1"), ("c", "k1"), ("d", 5, 3),
+    ("c", "m1"), ("c", "a10"), ("c", "a11"), ("c", "a12"), ("c", "a13"), ("c", "p1"),
+    ("c", "n1"), ("t", 1),
 )
 
 
@@ -104,11 +104,9 @@
         cp.start()
 
     barrier = pltpu.get_barrier_semaphore()
-    for k in range(1, NZ):
-        pl.semaphore_signal(barrier, inc=1, device_id={"seq": dev(y, zoff(k), c)}, device_id_type=MESH)
-    for peer in (partner, diag, near, far, nxt, prv, right, left):
+    for peer in (fwd, bwd, partner, diag, near, far, nxt, prv, right, left):
         pl.semaphore_signal(barrier, inc=1, device_id=peer, device_id_type=MESH)
-    pl.semaphore_wait(barrier, NZ - 1 + 8)
+    pl.semaphore_wait(barrier, 10)
 
     def piece(si, yy, zz, kind):
         layer, part = si // 3, si % 3
@@ -333,12 +331,11 @@
 
     def start_rest():
         loc[1].wait()
-        halo0.start()
         loc[2].wait()
         loc[3].wait()
         for layer in range(LAYERS):
             share = lax.dot_general(
-                WP[layer], PT[...], (((0,), (0,)), ((), ())), preferred_element_type=F32
+                WP[layer], PT[...], (((1,), (0,)), ((), ())), preferred_element_type=F32
             )
             POW[layer, y, z, c, :, 0:256] = share.astype(BF)
         for cp in loc[4:]:
@@ -353,6 +350,8 @@
             handlers[kind](*at)
         if n == 1:
             start_rest()
+        if ORDER[n] == ("f", 1, 4):
+            halo0.start()
 
     hv = (pl.ds(0, BLK // 2), pl.ds(BLK // 2, BLK // 2))
 
@@ -486,7 +485,7 @@
             pltpu.VMEM((2 * NZ, BLK), F32),
             pltpu.VMEM((NZ, 2 * NZ, BLK), F32),
             pltpu.VMEM((4, NZ, BLK), F32),
-            pltpu.VMEM((LAYERS, D, SHARD), BF),
+            pltpu.VMEM((LAYERS, SHARD, D), BF),
             pltpu.VMEM((D, 2 * BLK), BF),
             DMA((7,)),
             DMA((6, 7)),
@@ -509,7 +508,7 @@
             collective_id=0, has_side_effects=True, vmem_limit_bytes=58 * 1024 * 1024
         ),
     )(
-        embedded, w_qkv, w_out, w_pos, pos_table_t(2 * BLK, D), bias_content, bias_position, norm_gain, norm_offset,
+        embedded, w_qkv, w_out, jnp.swapaxes(w_pos, 1, 2), pos_table_t(2 * BLK, D), bias_content, bias_position, norm_gain, norm_offset,
         table, targets.reshape(32, BLK), valid_length,
     )
     return hidden, token_loss.reshape(BLK), loss[0, :1]

time: 108 us -> 106 us (0.981)
  local copies, waits for them, and re-layouts: 4.2 us -> 2.35 us
    unnamed x7 -> x6, local copies, waits for them, and re-layouts: 4.2 us -> 2.35 us
where the time goes in v3:
time: 106 us; the launch traced here: 105 us
  Pallas kernels  101 us (95%)
  between operations  2.46 us (2%)
  local copies, waits for them, and re-layouts  2.35 us (2%)
    pallas_call x1, Pallas kernels, on_device(): pl.pallas_call(kernel, out_shape=(jax.ShapeDtypeStruct((BLK, D), BF), jax...  101 us
    unnamed x6, local copies, waits for them, and re-layouts  2.35 us

profile of v3, /device:TPU:1, one launch (start us, length us, event | category | flops | bytes accessed | tf_op | source)
XLA Modules:
  0.0 105.5 jit_solution(207076117212181851)
XLA Ops:
  1.3 100.7 %shard_map.139 = (bf16[128,1024]{1,0:T(8,128)(2,1)}, f32[1,128]{1,0:T(1,128)}, f32[1,128]{1,0:T(1,128)}) custom-call(bf16[128,1024]{1,0:T(8,128)(2,1)} %emb.1, bf16[2,32,3072]{2,1,0:T(8,128)(2,1)} %wqkv.1, bf16[2,32,1024]{2,1,0:T(8,128)(2,1)} %w_out.1, bf16[2,32,1024]{2,1,0:T(8,128)(2,1)} %bitcast.5, bf16[1024,256]{1,0:T(8,128)(2,1)} %constant.5.ptab, ...), custom_call_target="tpu_custom_call" | custom-call | tf_op jit(solution)/shard_map/pallas_call | solution.py:463
  102.0 0.0 copy-start.1
  102.0 1.7 %copy.19 = bf16[128,1024]{1,0:T(8,128)(2,1)} copy(bf16[128,1024]{1,0:T(8,128)(2,1)} %get-tuple-element.12) | data formatting | bytes 524288
  103.7 0.0 copy-done.1
  103.7 0.0 copy-start
  103.7 0.5 copy.20
  104.2 0.2 copy-done
Async XLA Ops:
  102.0 1.7 %copy-start.1 = (f32[1,128]{1,0:T(1,128)S(1)}, f32[1,128]{1,0:T(1,128)}, u32[]{:S(2)}) copy-start(f32[1,128]{1,0:T(1,128)} %get-tuple-element.7) | copy-start | bytes 1540
  103.7 0.7 copy-start

commit v4 on v3

--- a/solution.py
+++ b/solution.py
@@ -26,21 +26,22 @@
     ("o", 0), ("o", 1), ("o", 2), ("f", 0, 1), ("b", 0, 1), ("y", 0, 0), ("f", 1, 1),
     ("b", 1, 1), ("f", 2, 1), ("b", 2, 1), ("y", 2, 0), ("y", 0, 4), ("f", 0, 2), ("b", 0, 2),
     ("y", 0, 1), ("f", 1, 2), ("b", 1, 2), ("y", 2, 4), ("f", 2, 2), ("b", 2, 2), ("y", 2, 1),
-    ("y", 0, 5), ("f", 0, 3), ("b", 0, 3), ("y", 0, 2), ("o", 3), ("f", 1, 3), ("b", 1, 3),
-    ("y", 2, 5), ("f", 2, 3), ("b", 2, 3), ("y", 2, 2), ("y", 0, 6), ("f", 0, 4), ("y", 0, 3),
-    ("d", 0, 0), ("b", 3, 1), ("f", 3, 1), ("o", 4), ("o", 5), ("f", 1, 4), ("d", 1, 0),
-    ("y", 3, 0), ("f", 2, 4), ("d", 2, 0), ("y", 2, 6), ("b", 3, 2), ("y", 0, 7), ("d", 0, 1),
-    ("y", 2, 3), ("f", 3, 2), ("b", 4, 1), ("d", 0, 2), ("y", 3, 4), ("y", 3, 1), ("b", 5, 1),
-    ("f", 4, 1), ("d", 1, 1), ("d", 2, 2), ("f", 5, 1), ("b", 3, 3), ("y", 2, 7), ("d", 2, 1),
-    ("y", 5, 0), ("f", 3, 3), ("d", 0, 3), ("b", 4, 2), ("y", 3, 5), ("y", 3, 2), ("b", 5, 2),
-    ("f", 4, 2), ("f", 5, 2), ("c", "q0"), ("c", "v0"), ("f", 3, 4), ("d", 3, 0), ("d", 2, 3),
-    ("b", 4, 3), ("y", 5, 1), ("y", 5, 4), ("y", 3, 6), ("b", 5, 3), ("f", 4, 3), ("y", 3, 3),
-    ("f", 5, 3), ("c", "a00"), ("c", "a01"), ("y", 5, 5), ("c", "a02"), ("f", 4, 4),
-    ("d", 4, 0), ("y", 5, 2), ("c", "a03"), ("y", 3, 7), ("d", 3, 2), ("d", 3, 1), ("f", 5, 4),
-    ("d", 5, 0), ("t", 0), ("c", "p0"), ("c", "n0"), ("y", 5, 3), ("y", 5, 6), ("d", 4, 1),
-    ("d", 3, 3), ("d", 5, 2), ("y", 5, 7), ("d", 5, 1), ("c", "q1"), ("c", "k1"), ("d", 5, 3),
-    ("c", "m1"), ("c", "a10"), ("c", "a11"), ("c", "a12"), ("c", "a13"), ("c", "p1"),
-    ("c", "n1"), ("t", 1),
+    ("y", 0, 5), ("f", 0, 3), ("b", 0, 3), ("y", 0, 2), ("f", 1, 3), ("b", 1, 3), ("o", 3),
+    ("y", 2, 5), ("f", 2, 3), ("b", 2, 3), ("y", 2, 2), ("f", 0, 4), ("d", 0, 0), ("y", 0, 6),
+    ("y", 0, 3), ("f", 1, 4), ("d", 1, 0), ("o", 5), ("b", 3, 1), ("f", 3, 1), ("y", 2, 6),
+    ("f", 2, 4), ("d", 2, 0), ("o", 4), ("y", 3, 0), ("d", 0, 2), ("f", 5, 1), ("b", 5, 1),
+    ("y", 0, 7), ("d", 0, 1), ("y", 2, 3), ("b", 3, 2), ("d", 1, 1), ("f", 3, 2), ("o", 6),
+    ("y", 3, 1), ("b", 4, 1), ("b", 5, 2), ("y", 3, 4), ("f", 4, 1), ("f", 5, 2), ("d", 2, 2),
+    ("b", 3, 3), ("y", 2, 7), ("d", 2, 1), ("d", 0, 3), ("b", 6, 1), ("f", 3, 3), ("y", 3, 2),
+    ("y", 3, 5), ("f", 6, 1), ("b", 4, 2), ("y", 6, 0), ("b", 5, 3), ("c", "q0"), ("f", 4, 2),
+    ("c", "v0"), ("d", 2, 3), ("f", 3, 4), ("d", 3, 0), ("f", 5, 3), ("b", 6, 2), ("y", 3, 6),
+    ("f", 6, 2), ("y", 3, 3), ("b", 4, 3), ("y", 6, 4), ("c", "a00"), ("f", 4, 3), ("y", 6, 1),
+    ("c", "a01"), ("f", 5, 4), ("d", 5, 0), ("c", "a02"), ("f", 6, 3), ("b", 6, 3),
+    ("c", "a03"), ("y", 3, 7), ("d", 3, 1), ("d", 3, 2), ("c", "p0"), ("y", 6, 2), ("f", 4, 4),
+    ("d", 4, 0), ("c", "n0"), ("y", 6, 5), ("f", 6, 4), ("d", 6, 0), ("t", 0), ("y", 6, 3),
+    ("d", 5, 1), ("y", 6, 6), ("d", 3, 3), ("d", 4, 1), ("d", 6, 2), ("y", 6, 7), ("d", 6, 1),
+    ("c", "q1"), ("c", "k1"), ("c", "m1"), ("c", "a10"), ("d", 6, 3), ("c", "a11"),
+    ("c", "a12"), ("c", "a13"), ("c", "p1"), ("c", "n1"),
 )
 
 
@@ -109,17 +110,20 @@
     pl.semaphore_wait(barrier, 10)
 
     def piece(si, yy, zz, kind):
-        layer, part = si // 3, si % 3
-        if part == 2:
-            at, size = {"ring": (xp * 384, 896), "give": (xp * 896, 384), "take": ((1 - xp) * 896, 384)}[kind]
-            return POW.at[layer, yy, zz, c, :, pl.ds(pl.multiple_of(at, 128), size)]
-        if part == 1:
+        layer = si // 3 if si < 6 else 1
+        if si == 5:
+            return POW.at[1, yy, zz, c, :, pl.ds(0, 256)]
+        if si in (2, 6):
+            first, wide = (0, 896) if si == 2 else (256, 640)
+            at, size = {"ring": (xp * 384, wide), "give": (xp * wide, 384), "take": ((1 - xp) * wide, 384)}[kind]
+            return POW.at[layer, yy, zz, c, :, pl.ds(pl.multiple_of(first + at, 128), size)]
+        if si % 3 == 1:
             return W.at[layer, yy, zz, c, :, pl.ds(D, D)]
         at = (1 - xp if kind == "take" else xp) * 2 * D
         return W.at[layer, yy, zz, c, :, pl.ds(pl.multiple_of(at, D), D)]
 
     def shares(si):
-        return si % 3 != 1
+        return si in (0, 2, 3, 6)
 
     def place(k):
         return zoff(sgn * k) if k < 4 else zoff(-sgn * (k - 3))
@@ -322,6 +326,8 @@
                 finish(2 + 3 * layer)
             attend(layer, 2 * k, 2 * k + 2)
         elif kind == "p":
+            if layer == 1:
+                finish(6)
             project(layer, X)
         elif name == "n0":
             norm(0, X1.at[1], False)
@@ -368,8 +374,7 @@
         hcopy(0, False, half).start()
         hcopy(0, True, half).start()
 
-    tcopies[2].wait_recv()
-    t_other.wait_recv()
+    table_step(1)
 
     def stats(slot, blocks):
         n = len(blocks)
@@ -394,7 +399,6 @@
             STL[pl.ds(zz, 1), :] = sums[:, k * BLK : (k + 1) * BLK]
             STL[pl.ds(NZ + zz, 1), :] = picks[:, k * BLK : (k + 1) * BLK]
 
-    stats(0, [z])
     for d in (1, 2, 3, 4):
         for half in (0, 1):
             hcopy(d - 1, False, half).wait_recv()
@@ -403,6 +407,10 @@
                 hcopy(d - 1, True, half).wait_recv()
                 if d < 3:
                     hcopy(d, True, half).start()
+        if d == 1:
+            tcopies[2].wait_recv()
+            t_other.wait_recv()
+            stats(0, [z])
         if d < 4:
             stats(2 * d - 1, [zoff(-sgn * d), zoff(sgn * d)])
         else:
@@ -441,7 +449,7 @@
 
     for cp in pc + scopies:
         cp.wait_send()
-    for si in range(6):
+    for si in range(7):
         drain(si)
     halo0.wait_send()
     halo1.wait_send()
@@ -488,11 +496,11 @@
             pltpu.VMEM((LAYERS, SHARD, D), BF),
             pltpu.VMEM((D, 2 * BLK), BF),
             DMA((7,)),
-            DMA((6, 7)),
-            DMA((6, 8)),
-            DMA((6, 4)),
-            DMA((6, 4)),
-            DMA((6, 10)),
+            DMA((7, 7)),
+            DMA((7, 8)),
+            DMA((7, 4)),
+            DMA((7, 4)),
+            DMA((7, 10)),
             DMA((2,)),
             DMA((2,)),
             DMA((4,)),

time: 106 us -> 106 us (level)
  no operation moved by 1% of the time
where the time goes in v4:
time: 106 us
  Pallas kernels  101 us (95%)
  between operations  2.46 us (2%)
  local copies, waits for them, and re-layouts  2.35 us (2%)
    pallas_call x1, Pallas kernels, on_device(): pl.pallas_call(kernel, out_shape=(jax.ShapeDtypeStruct((BLK, D), BF), jax...  101 us
    unnamed x6, local copies, waits for them, and re-layouts  2.35 us

profile of v4, /device:TPU:1, one launch (start us, length us, event | category | flops | bytes accessed | tf_op | source)
XLA Modules:
  0.0 106.1 jit_solution(13576816582858632061)
XLA Ops:
  1.3 101.2 %shard_map.139 = (bf16[128,1024]{1,0:T(8,128)(2,1)}, f32[1,128]{1,0:T(1,128)}, f32[1,128]{1,0:T(1,128)}) custom-call(bf16[128,1024]{1,0:T(8,128)(2,1)} %emb.1, bf16[2,32,3072]{2,1,0:T(8,128)(2,1)} %wqkv.1, bf16[2,32,1024]{2,1,0:T(8,128)(2,1)} %w_out.1, bf16[2,32,1024]{2,1,0:T(8,128)(2,1)} %bitcast.5, bf16[1024,256]{1,0:T(8,128)(2,1)} %constant.5.ptab, ...), custom_call_target="tpu_custom_call" | custom-call | tf_op jit(solution)/shard_map/pallas_call | solution.py:471
  102.5 0.0 copy-start.1
  102.5 1.7 %copy.19 = bf16[128,1024]{1,0:T(8,128)(2,1)} copy(bf16[128,1024]{1,0:T(8,128)(2,1)} %get-tuple-element.12) | data formatting | bytes 524288
  104.2 0.0 copy-done.1
  104.2 0.0 copy-start
  104.2 0.5 copy.20
  104.7 0.2 copy-done
Async XLA Ops:
  102.5 1.7 %copy-start.1 = (f32[1,128]{1,0:T(1,128)S(1)}, f32[1,128]{1,0:T(1,128)}, u32[]{:S(2)}) copy-start(f32[1,128]{1,0:T(1,128)} %get-tuple-element.7) | copy-start | bytes 1540
  104.2 0.7 copy-start

commit v5 on v4

--- a/solution.py
+++ b/solution.py
@@ -268,6 +268,17 @@
 
         lax.fori_loop(0, 4, body, 0)
 
+    hv = [pl.ds(k * BLK // 4, BLK // 4) for k in range(4)]
+
+    def hcopy(d, backward, half):
+        src = 0 if d == 0 else (2 * d if backward else 2 * d - 1)
+        dst = 2 * d + 2 if backward else 2 * d + 1
+        k = (4 if backward else 0) + d
+        return rcopy(
+            HALL.at[src, hv[half]], HALL.at[dst, hv[half]],
+            h_s.at[1 if backward else 0], h_r.at[k, half], bwd if backward else fwd,
+        )
+
     def norm(layer, dst, last):
         def body(t, carry):
             r = pl.ds(pl.multiple_of(t * 32, 32), 32)
@@ -281,7 +292,15 @@
                 hid_out[r, :] = jnp.where(pos < vlen[0], h, 0.0).astype(BF)
             return carry
 
-        lax.fori_loop(0, 4, body, 0)
+        if not last:
+            lax.fori_loop(0, 4, body, 0)
+            return
+        for t in range(5):
+            if t < 4:
+                body(t, 0)
+            if t > 0:
+                hcopy(0, False, t - 1).start()
+                hcopy(0, True, t - 1).start()
 
     halves = (pl.ds(0, WORDS // 2), pl.ds(WORDS // 2, WORDS // 2))
     tcopies = [
@@ -359,21 +378,6 @@
         if ORDER[n] == ("f", 1, 4):
             halo0.start()
 
-    hv = (pl.ds(0, BLK // 2), pl.ds(BLK // 2, BLK // 2))
-
-    def hcopy(d, backward, half):
-        src = 0 if d == 0 else (2 * d if backward else 2 * d - 1)
-        dst = 2 * d + 2 if backward else 2 * d + 1
-        k = (4 if backward else 0) + d
-        return rcopy(
-            HALL.at[src, hv[half]], HALL.at[dst, hv[half]],
-            h_s.at[1 if backward else 0], h_r.at[k, half], bwd if backward else fwd,
-        )
-
-    for half in (0, 1):
-        hcopy(0, False, half).start()
-        hcopy(0, True, half).start()
-
     table_step(1)
 
     def stats(slot, blocks):
@@ -400,7 +404,7 @@
             STL[pl.ds(NZ + zz, 1), :] = picks[:, k * BLK : (k + 1) * BLK]
 
     for d in (1, 2, 3, 4):
-        for half in (0, 1):
+        for half in range(4):
             hcopy(d - 1, False, half).wait_recv()
             if d < 4:
                 hcopy(d, False, half).start()
@@ -506,7 +510,7 @@
             DMA((4,)),
             DMA((4,)),
             DMA((2,)),
-            DMA((7, 2)),
+            DMA((7, 4)),
             DMA((NZ - 1,)),
             DMA((NZ - 1,)),
             DMA((3,)),

time: 106 us -> 105 us (level)
    pallas_call x1, Pallas kernels: 101 us -> 100 us  [on_device(): pl.pallas_call(kernel, out_shape=(jax.ShapeDtypeStruct((BLK, D), BF), jax...]
where the time goes in v5:
time: 105 us
  Pallas kernels  100 us (95%)
  between operations  2.46 us (2%)
  local copies, waits for them, and re-layouts  2.35 us (2%)
    pallas_call x1, Pallas kernels, on_device(): pl.pallas_call(kernel, out_shape=(jax.ShapeDtypeStruct((BLK, D), BF), jax...  100 us
    unnamed x6, local copies, waits for them, and re-layouts  2.35 us

profile of v5, /device:TPU:1, one launch (start us, length us, event | category | flops | bytes accessed | tf_op | source)
XLA Modules:
  0.0 104.9 jit_solution(18346457674855062056)
XLA Ops:
  1.3 100.1 %shard_map.139 = (bf16[128,1024]{1,0:T(8,128)(2,1)}, f32[1,128]{1,0:T(1,128)}, f32[1,128]{1,0:T(1,128)}) custom-call(bf16[128,1024]{1,0:T(8,128)(2,1)} %emb.1, bf16[2,32,3072]{2,1,0:T(8,128)(2,1)} %wqkv.1, bf16[2,32,1024]{2,1,0:T(8,128)(2,1)} %w_out.1, bf16[2,32,1024]{2,1,0:T(8,128)(2,1)} %bitcast.5, bf16[1024,256]{1,0:T(8,128)(2,1)} %constant.5.ptab, ...), custom_call_target="tpu_custom_call" | custom-call | tf_op jit(solution)/shard_map/pallas_call | solution.py:475
  101.3 0.0 copy-start.1
  101.4 1.7 %copy.19 = bf16[128,1024]{1,0:T(8,128)(2,1)} copy(bf16[128,1024]{1,0:T(8,128)(2,1)} %get-tuple-element.12) | data formatting | bytes 524288
  103.0 0.0 copy-done.1
  103.0 0.0 copy-start
  103.0 0.5 copy.20
  103.5 0.2 copy-done
Async XLA Ops:
  101.3 1.7 %copy-start.1 = (f32[1,128]{1,0:T(1,128)S(1)}, f32[1,128]{1,0:T(1,128)}, u32[]{:S(2)}) copy-start(f32[1,128]{1,0:T(1,128)} %get-tuple-element.7) | copy-start | bytes 1540
  103.0 0.7 copy-start
